TPU v7x, 256 devices: a whole 4x4x8 slice. The times are simulated.
256 devices in a mesh: gz: 64 (over y, z, core), ga: 4 (over x).
Axes of the slice: x: 4, y: 4, z: 8, core: 2. Of those that a mesh axis runs over, the one named last changes fastest.
Arguments:
- solution: float32 [512, 256, 256], P(('gz', 'ga')), may hold values from -6 to 6
- residual: float32 [512, 256, 256], P(('gz', 'ga')), may hold values from -40 to 40
- direction: float32 [512, 256, 256], P(('gz', 'ga')), may hold values from -40 to 40
Outputs:
- solution_out: float32 [512, 256, 256], P(('gz', 'ga'))
- residual_out: float32 [512, 256, 256], P(('gz', 'ga'))
- direction_out: float32 [512, 256, 256], P(('gz', 'ga'))
All inputs are finite; a program needn't handle non-finite values.
Results may differ from a plain program's by a relative error of at most 0.0003.
Values sent between devices are 32-bit elements; how exact they have to be, the bound alone decides.
No kernel may reach another device: no remote copies, remote signals or barrier semaphores. Data moves between devices by JAX's collectives and lax.ppermute only.
A program may use at most 128 MiB of HBM per device.

v0:
```python
import functools

import jax
import jax.numpy as jnp
from jax import lax
from jax.experimental import pallas as pl
from jax.experimental.pallas import tpu as pltpu
from jax.sharding import Mesh, PartitionSpec as P


S = 8
PIECES = 4
COLS = 2 * S + 1
PLANES = 8
HALO = 8
TALL = PLANES + 2 * HALO
PAD = 8
HALF = 128
GROUP = 4
FIRST = -1.0 / 6.0
NEXT = -1.0 / 3.0
ALL = ("zz", "c", "x")
VMEM = pl.BlockSpec(memory_space=pltpu.VMEM)
HBM = pl.BlockSpec(memory_space=pltpu.HBM)

DD, RR, DR = 0, 2 * S + 1, 4 * S
SUMS = 6 * S


def here():
    return lax.axis_index("c"), lax.axis_index("x")


def piece_of(k):
    return (lax.axis_index("x") + k) % PIECES


def chain_plan(steps):
    lows = [0] + [HALO - steps + k for k in range(1, steps + 1)]
    ends = [TALL] + [HALO + PLANES + steps - k for k in range(1, steps + 1)]
    return lows, ends


def parting(back):
    i = lax.broadcasted_iota(jnp.int32, (2 * HALF, 2 * HALF), 0 if back else 1)
    j = lax.broadcasted_iota(jnp.int32, (2 * HALF, 2 * HALF), 1 if back else 0)
    return (j == jnp.where(i < HALF, 2 * i, 2 * (i - HALF) + 1)).astype(jnp.float32)


def move_columns(value, matrix):
    return jnp.dot(value, matrix, precision=lax.Precision.HIGHEST, preferred_element_type=jnp.float32)


def pack_kernel(source, *refs):
    outs, hold = refs[:PIECES], refs[PIECES]
    per, halves, rows, _ = outs[0].shape
    keep, height = rows - 2 * HALO, source.shape[1]
    matrix = parting(False)
    for plane in range(per):
        parted = move_columns(source[plane], matrix)
        for h in range(halves):
            hold[plane, h] = parted[:, h * HALF : (h + 1) * HALF]
    for k in range(PIECES):
        g = piece_of(k)
        row = pl.multiple_of(g * keep, keep)
        below = pl.multiple_of(jnp.maximum(row - HALO, 0), HALO)
        above = pl.multiple_of(jnp.minimum(row + keep, height - HALO), HALO)
        has_below, has_above = (g != 0).astype(jnp.float32), (g != PIECES - 1).astype(jnp.float32)
        for plane in range(per):
            for h in range(halves):
                outs[k][plane, h, :HALO] = hold[plane, h, pl.ds(below, HALO)] * has_below
                outs[k][plane, h, pl.ds(HALO, keep)] = hold[plane, h, pl.ds(row, keep)]
                outs[k][plane, h, rows - HALO :] = hold[plane, h, pl.ds(above, HALO)] * has_above


def join_kernel(*refs):
    out = refs[PIECES]
    core, _ = here()
    per = refs[0].shape[0]
    for k in range(PIECES):
        plane = per * piece_of(PIECES - k)
        for p in range(per):
            out[jnp.where(core == 0, plane + p, PLANES - 1 - plane - p)] = refs[k][p]


def load_planes(chain, source, places):
    rows = pl.ds(PAD, source.shape[2])
    for i, place in enumerate(places):
        for h in range(2):
            chain[0][place, h, rows] = source[i, h]


def run_groups(groups, chain, sideways, rows, steps):
    lows, _ = chain_plan(steps)
    data = pl.ds(PAD, rows)
    core, x = here()
    zz = lax.axis_index("zz")
    last = lax.axis_size("zz") - 1
    alone = jnp.logical_or(jnp.logical_and(zz == 0, core == 0), jnp.logical_and(zz == last, core == 1))
    low_x = (x != 0).astype(jnp.float32)
    high_x = (x != PIECES - 1).astype(jnp.float32)
    across_valid = 1.0 - alone.astype(jnp.float32)
    lane = lax.broadcasted_iota(jnp.int32, (rows, HALF), 1)
    at_low, at_high = lane == 0, lane == HALF - 1

    def neighbours_y(power, plane):
        source = chain[power - 1]
        index = plane - lows[power - 1]
        a, b = source[index, 0, data], source[index, 1, data]
        first = b + jnp.where(at_low, 0.0, pltpu.roll(b, 1, 1))
        second = a + jnp.where(at_high, 0.0, pltpu.roll(a, HALF - 1, 1))
        return first, second

    def value(power, plane, slot, across):
        now, new = chain[power - 1], chain[power]
        index = plane - lows[power - 1]
        scale = FIRST if power == 1 else NEXT
        if across:
            scale = scale * across_valid
        for h in range(2):
            total = now[index - 1, h, data] + now[index + 1, h, data]
            total = total + (now[index, h, pl.ds(PAD - 1, rows)] + now[index, h, pl.ds(PAD + 1, rows)])
            total = total + sideways[slot, h]
            parts = []
            for a, b, weight in ((0, HALO, low_x), (HALO, rows - HALO, None), (rows - HALO, rows, high_x)):
                parts.append(total[a:b] * (scale if weight is None else scale * weight))
            result = jnp.concatenate(parts, axis=0)
            if power > 1:
                result = result - chain[power - 2][plane - lows[power - 2], h, data]
            new[plane - lows[power], h, data] = result

    def step(group, then):
        power, plane, count = group
        made = [(power, plane + u) for u in range(count)] if isinstance(plane, int) else []
        ahead, late = [], []
        if then:
            for u in range(then[2]):
                if (then[0] - 1, then[1] + u) in made:
                    late.append(u)
                else:
                    ahead.append((u, neighbours_y(then[0], then[1] + u)))
        for u in range(count):
            value(power, plane + u, u, isinstance(plane, int) and plane + u < HALO)
        ahead += [(u, neighbours_y(then[0], then[1] + u)) for u in late]
        for u, pair in ahead:
            sideways[u, 0], sideways[u, 1] = pair

    first = groups[0]
    for u in range(first[2]):
        sideways[u, 0], sideways[u, 1] = neighbours_y(first[0], first[1] + u)
    at = 0
    while at < len(groups):
        power, plane, count = groups[at]
        run = 0
        while at + run + 1 < len(groups) and groups[at + run + 1] == (power, plane + GROUP * (run + 1), count) and count == GROUP:
            run += 1
        if run >= 2:

            def body(g, _, power=power, plane=plane):
                now = plane + GROUP * g
                step((power, now, GROUP), (power, now + GROUP, GROUP))
                return 0

            lax.fori_loop(0, run, body, 0)
            at += run
        step(groups[at], groups[at + 1] if at + 1 < len(groups) else None)
        at += 1


def near_groups(steps):
    _, ends = chain_plan(steps)
    groups = []
    for power in range(1, steps + 1):
        low, end = HALO + power, ends[power]
        left = end - low
        while left > 0:
            count = min(GROUP, left)
            if left in (5, 6):
                count = 3
            groups.append((power, low, count))
            low, left = low + count, left - count
    return groups


def far_groups(steps):
    lows, _ = chain_plan(steps)
    groups = []
    for power in range(1, steps + 1):
        middle = HALO + power - GROUP
        groups.append((power, middle, GROUP))
        groups.append((power, lows[power], middle - lows[power]))
    return groups


def near_kernel(steps, own, side, *refs):
    chain, sideways = refs[: steps + 1], refs[steps + 1]
    load_planes(chain, own, range(HALO, HALO + PLANES))
    load_planes(chain, side, range(TALL - 1, HALO + PLANES - 1, -1))
    run_groups(near_groups(steps), chain, sideways, own.shape[2], steps)


def add_products(acc, chain, steps, other, keep):
    rows = pl.ds(PAD + HALO, keep)
    acc[...] = jnp.zeros_like(acc)

    def total(a, b):
        return jnp.sum((a * b).reshape(keep // 8, 8, HALF), axis=0)

    def body(step, _):
        plane, h = step // 2, step % 2

        def of(chain, steps, k):
            return chain[k][HALO + plane - chain_plan(steps)[0][k], h, rows]

        before, beside = None, None
        if other:
            beside = of(other, S, 0)
        for k in range(steps + 1):
            now = of(chain, steps, k)
            acc[2 * k] += total(now, now)
            if k:
                acc[2 * k - 1] += total(before, now)
            if other:
                following = of(other, S, k + 1)
                acc[2 * steps + 1 + 2 * k] += total(beside, now)
                acc[2 * steps + 2 + 2 * k] += total(following, now)
                beside = following
            before = now
        return 0

    lax.fori_loop(0, 2 * PLANES, body, 0)


def put_products(acc, parts, place):
    for k in range(acc.shape[0]):
        parts[pl.ds(place + k, 1), :] = jnp.sum(acc[k], axis=0, keepdims=True)


def far_direction_kernel(across, *refs):
    chain, parts, sideways, acc = refs[S + 1 : 2 * S + 2], refs[2 * S + 2], refs[2 * S + 3], refs[2 * S + 4]
    rows = across.shape[2]
    load_planes(chain, across, range(HALO - 1, HALO - 1 - across.shape[0], -1))
    run_groups(far_groups(S), chain, sideways, rows, S)
    add_products(acc, chain, S, None, rows - 2 * HALO)
    parts[...] = jnp.zeros_like(parts)
    put_products(acc, parts, DD)


def far_residual_kernel(across, *refs):
    other, parts_d, refs = refs[: S + 1], refs[S + 1], refs[S + 2 :]
    chain, sums, sideways, acc, parts = refs[S : 2 * S], refs[2 * S], refs[2 * S + 1], refs[2 * S + 2], refs[2 * S + 3]
    rows = across.shape[2]
    load_planes(chain, across, range(HALO - 1, HALO - 1 - across.shape[0], -1))
    run_groups(far_groups(S - 1), chain, sideways, rows, S - 1)
    add_products(acc, chain, S - 1, other, rows - 2 * HALO)
    parts[...] = parts_d[...]
    put_products(acc, parts, RR)
    sums[...] = jnp.sum(parts[...].T, axis=0, keepdims=True)


def coefficients(sums):
    tall = 24
    shape = (tall, 128)
    i = lax.broadcasted_iota(jnp.int32, shape, 0)
    j = lax.broadcasted_iota(jnp.int32, shape, 1)
    row_r, col_r = i > S, j > S
    a = jnp.where(row_r, i - (S + 1), i)
    b = jnp.where(col_r, j - (S + 1), j)
    valid = jnp.logical_and(i < COLS, j < COLS)
    base = jnp.where(row_r, jnp.where(col_r, RR, DR), jnp.where(col_r, DR, DD))
    at_plus = jnp.where(valid, base + a + b, -1)
    at_minus = jnp.where(valid, base + jnp.abs(a - b), -1)
    at_base = jnp.where(valid, base + ((a + b) & 1), -1)
    gram = jnp.zeros(shape, jnp.float32)
    for place in range(SUMS):
        weight = (
            (at_plus == place).astype(jnp.float32)
            + (at_minus == place).astype(jnp.float32)
            - (at_base == place).astype(jnp.float32)
        )
        gram = gram + weight * sums[:, place : place + 1]

    def change(index, axis):
        second = index > S
        k = jnp.where(second, index - (S + 1), index)
        count = jnp.where(second, S, S + 1)
        valid = index < COLS
        middle = jnp.where(jnp.logical_and(valid, k < count - 1), 6.0, 0.0)
        below = jnp.where(jnp.logical_and(valid, k >= 1), jnp.where(k == 1, 6.0, 3.0), 0.0)
        above = jnp.where(jnp.logical_and(valid, k + 1 < count - 1), 3.0, 0.0)
        size = shape[axis]

        def apply(v):
            return middle * v + below * pltpu.roll(v, 1, axis) + above * pltpu.roll(v, size - 1, axis)

        return apply

    down, along = change(i, 0), change(j, 1)

    def quadratic(left_down, right_along):
        return jnp.sum(left_down * (gram * right_along), keepdims=True)

    def unit(index, k):
        return (index == k).astype(jnp.float32)

    q_d, q_a = unit(i, 0), unit(j, 0)
    w_d, w_a = unit(i, S + 1), unit(j, S + 1)
    c_d = jnp.zeros(shape, jnp.float32)
    rho = quadratic(w_d, w_a)
    for _ in range(S):
        m_d, m_a = down(q_d), along(q_a)
        alpha = rho / quadratic(q_d, m_a)
        c_d = c_d + alpha * q_d
        w_d, w_a = w_d - alpha * m_d, w_a - alpha * m_a
        rho_new = quadratic(w_d, w_a)
        beta = rho_new / rho
        q_d, q_a = w_d + beta * q_d, w_a + beta * q_a
        rho = rho_new
    return c_d, w_d, q_d


def combine(k, coefs, chain_d, chain_r, out, hold):
    per, keep = out.shape[1], out.shape[2]
    core, _ = here()
    first = per * piece_of(k)
    tile = 16

    def body(step, _):
        plane, at = step // (keep // tile), step % (keep // tile)
        row = pl.multiple_of(at * tile, tile)
        source = pl.ds(pl.multiple_of(PAD + HALO + row, 8), tile)
        where = HALO + jnp.where(core == 0, first + plane, PLANES - 1 - first - plane)
        sums = [[None] * 3, [None] * 3]
        for column in range(COLS):
            chain, power, steps = (chain_d, column, S) if column <= S else (chain_r, column - S - 1, S - 1)
            low = chain_plan(steps)[0][power]
            factors = [coefs[which, column : column + 1, :] for which in range(3)]
            for h in range(2):
                v = chain[power][where - low, h, source]
                for which in range(3):
                    term = v * factors[which]
                    sums[h][which] = term if column == 0 else sums[h][which] + term
        for h in range(2):
            for which in range(3):
                to = pl.multiple_of((which * per + plane) * keep + row, tile)
                hold[pl.ds(to, tile), h * HALF : (h + 1) * HALF] = sums[h][which]
        return 0

    lax.fori_loop(0, per * (keep // tile), body, 0)
    out[...] = move_columns(hold[...], parting(True)).reshape(out.shape)


def first_combine_kernel(k, sums, *refs):
    chain_d, chain_r, out, coefs, hold = refs[: S + 1], refs[S + 1 : COLS], *refs[COLS:]
    total = jnp.sum(sums[...], axis=0, keepdims=True)
    for which, value in enumerate(coefficients(total)):
        coefs[which] = value
    combine(k, coefs, chain_d, chain_r, out, hold)


def combine_kernel(k, coefs, *refs):
    combine(k, coefs, refs[: S + 1], refs[S + 1 : COLS], *refs[COLS:])


def finish_kernel(solution, *refs):
    pieces, outs, hold, sem = refs[:PIECES], refs[PIECES : PIECES + 3], refs[PIECES + 3], refs[PIECES + 4]
    _, per, keep, _ = pieces[0].shape
    copies = []
    for which in (1, 2, 0):
        for k in range(PIECES):
            rows = pl.ds(pl.multiple_of(piece_of(PIECES - k) * keep, keep), keep)
            for plane in range(per):
                value = pieces[k][which, plane]
                if which == 0:
                    value = value + solution[plane, rows]
                hold[which, plane, rows] = value
        copies.append(pltpu.make_async_copy(hold.at[which], outs[which], sem.at[which]))
        copies[-1].start()
    for copy in copies:
        copy.wait()


def on_device(solution, residual, direction):
    groups = lax.axis_size("x")
    outer = lax.axis_size("zz")
    per, height, lanes = direction.shape
    keep = height // groups
    rows = keep + 2 * HALO
    f32 = jnp.float32

    blocks = 2 * outer
    near = [(b, b - 1) for b in range(0, blocks, 2) if b > 0] + [(b, b + 1) for b in range(1, blocks, 2) if b + 1 < blocks]

    def params(mib=4):
        return pltpu.CompilerParams(vmem_limit_bytes=mib * 2**20)

    def cost(us):
        return pl.CostEstimate(flops=us * 10**7, bytes_accessed=0, transcendentals=0)

    def ahead(value, k):
        return lax.ppermute(value, "x", [(i, (i + k) % groups) for i in range(groups)])

    def spread(field, reach):
        pieces = pl.pallas_call(
            pack_kernel,
            out_shape=(jax.ShapeDtypeStruct((per, 2, rows, HALF), f32),) * groups,
            in_specs=[VMEM],
            out_specs=(VMEM,) * groups,
            scratch_shapes=[pltpu.VMEM((per, 2, height, HALF), f32)],
            compiler_params=params(),
            name="pack",
        )(field)
        got = [pieces[0]]
        for k in range(1, groups):
            got.append(ahead(pieces[k], k))
        own = pl.pallas_call(
            join_kernel,
            out_shape=jax.ShapeDtypeStruct((PLANES, 2, rows, HALF), f32),
            in_specs=[VMEM] * groups,
            out_specs=VMEM,
            compiler_params=params(1),
            name="join",
        )(*got)
        side = lax.ppermute(own, "c", [(0, 1), (1, 0)])
        across = lax.ppermute(own[:reach], ("zz", "c"), near)
        return own, side, across

    def chain_shapes(steps):
        return tuple(
            jax.ShapeDtypeStruct((end - low, 2, rows + 2 * PAD, HALF), f32) for low, end in zip(*chain_plan(steps))
        )

    sideways = pltpu.VMEM((GROUP, 2, rows, HALF), f32)

    def near_chain(steps, own, side):
        return pl.pallas_call(
            functools.partial(near_kernel, steps),
            out_shape=chain_shapes(steps),
            in_specs=[VMEM] * 2,
            out_specs=(VMEM,) * (steps + 1),
            scratch_shapes=[sideways],
            compiler_params=params(),
            cost_estimate=cost(4),
            name="near_chain",
        )(own, side)

    own_d, side_d, across_d = spread(direction, S)
    own_r, side_r, across_r = spread(residual, S - 1)
    chain_d = near_chain(S, own_d, side_d)
    *chain_d, parts = pl.pallas_call(
        far_direction_kernel,
        out_shape=(*chain_shapes(S), jax.ShapeDtypeStruct((128, 128), f32)),
        in_specs=[VMEM] * (S + 2),
        out_specs=(VMEM,) * (S + 2),
        scratch_shapes=[sideways, pltpu.VMEM((2 * S + 1, 8, HALF), f32)],
        input_output_aliases={1 + k: k for k in range(S + 1)},
        compiler_params=params(),
        cost_estimate=cost(4),
        name="far_direction",
    )(across_d, *chain_d)
    chain_r = near_chain(S - 1, own_r, side_r)
    *chain_r, sums = pl.pallas_call(
        far_residual_kernel,
        out_shape=(*chain_shapes(S - 1), jax.ShapeDtypeStruct((1, 128), f32)),
        in_specs=[VMEM] * (2 * S + 3),
        out_specs=(VMEM,) * (S + 1),
        scratch_shapes=[sideways, pltpu.VMEM((4 * S - 1, 8, HALF), f32), pltpu.VMEM((128, 128), f32)],
        input_output_aliases={S + 3 + k: k for k in range(S)},
        compiler_params=params(),
        cost_estimate=cost(4),
        name="far_residual",
    )(across_r, *chain_d, parts, *chain_r)

    devices = groups * blocks
    everyone = lax.all_to_all(jnp.broadcast_to(sums[None], (devices, 1, 128)), ALL, 0, 0, tiled=True)

    mixed_shape = jax.ShapeDtypeStruct((3, per, keep, lanes), f32)
    hold = pltpu.VMEM((3 * per * keep, lanes), f32)
    mixed = {}
    first, *others = (2, 1, 3, 0)
    mixed[first], coefs = pl.pallas_call(
        functools.partial(first_combine_kernel, first),
        out_shape=(mixed_shape, jax.ShapeDtypeStruct((3, 24, 128), f32)),
        in_specs=[VMEM] * (COLS + 1),
        out_specs=(VMEM, VMEM),
        scratch_shapes=[hold],
        compiler_params=params(),
        cost_estimate=cost(4),
        name="combine",
    )(everyone.reshape(devices, 128), *chain_d, *chain_r)
    for k in others:
        mixed[k] = pl.pallas_call(
            functools.partial(combine_kernel, k),
            out_shape=mixed_shape,
            in_specs=[VMEM] * (COLS + 1),
            out_specs=VMEM,
            scratch_shapes=[hold],
            compiler_params=params(),
            cost_estimate=cost(1),
            name="combine",
        )(coefs, *chain_d, *chain_r)
    back = [mixed[0]]
    for k in range(1, groups):
        back.append(ahead(mixed[k], k))

    whole = jax.ShapeDtypeStruct((per, height, lanes), f32)
    return pl.pallas_call(
        finish_kernel,
        out_shape=(whole,) * 3,
        in_specs=[VMEM] * (groups + 1),
        out_specs=(HBM,) * 3,
        scratch_shapes=[pltpu.VMEM((3, per, height, lanes), f32), pltpu.SemaphoreType.DMA((3,))],
        compiler_params=params(8),
        name="finish",
    )(solution, *back)


def solution(mesh):
    blocks, groups = mesh.devices.shape
    split = Mesh(mesh.devices.reshape(blocks // 2, 2, groups), ALL)
    spec = P(ALL, None, None)

    return jax.shard_map(
        on_device, mesh=split, in_specs=(spec, spec, spec), out_specs=(spec, spec, spec), check_vma=False
    )
```

profile of v0, /device:TPU:1, one launch (start us, length us, event | category | flops | bytes accessed | tf_op | source)
XLA Modules:
  0.0 97.7 jit_solution(15545036204325020624)
XLA Ops:
  0.6 0.0 copy-start
  0.6 1.0 %copy-done = f32[2,256,256]{2,1,0:T(8,128)S(1)} copy-done((f32[2,256,256]{2,1,0:T(8,128)S(1)}, f32[2,256,256]{2,1,0:T(8,128)}, u32[]{:S(2)}) %copy-start) | copy-done | bytes 524312
  1.7 0.7 pack.3
  2.3 2.1 %collective-permute-start.4 = (f32[2,2,80,128]{3,2,1,0:T(8,128)S(1)}, f32[2,2,80,128]{3,2,1,0:T(8,128)S(1)}, u32[]{:S(2)}, u32[]{:S(2)}) collective-permute-start(f32[2,2,80,128]{3,2,1,0:T(8,128)S(1)} %get-tuple-element.54), channel_id=1, source_target_pairs={{0,1},{1,2},{2,3},{3,0},{4,5},{5,6},{6,7},{7,4},{8,9},{9,10},{10,1... | collective-permute-start | bytes 491528 | tf_op jit(solution)/shard_map/ppermute | solution.py:401
  4.4 2.5 %collective-permute-start.5 = (f32[2,2,80,128]{3,2,1,0:T(8,128)S(1)}, f32[2,2,80,128]{3,2,1,0:T(8,128)S(1)}, u32[]{:S(2)}, u32[]{:S(2)}) collective-permute-start(f32[2,2,80,128]{3,2,1,0:T(8,128)S(1)} %get-tuple-element.55), channel_id=1, source_target_pairs={{0,2},{1,3},{2,0},{3,1},{4,6},{5,7},{6,4},{7,5},{8,10},{9,11},{10,... | collective-permute-start | bytes 491528 | tf_op jit(solution)/shard_map/ppermute | solution.py:401
  6.9 1.2 %collective-permute-start.6 = (f32[2,2,80,128]{3,2,1,0:T(8,128)S(1)}, f32[2,2,80,128]{3,2,1,0:T(8,128)S(1)}, u32[]{:S(2)}, u32[]{:S(2)}) collective-permute-start(f32[2,2,80,128]{3,2,1,0:T(8,128)S(1)} %get-tuple-element.56), channel_id=1, source_target_pairs={{0,3},{1,0},{2,1},{3,2},{4,7},{5,4},{6,5},{7,6},{8,11},{9,8},{10,9... | collective-permute-start | bytes 491528 | tf_op jit(solution)/shard_map/ppermute | solution.py:401
  8.0 0.0 copy-start.1
  8.1 1.0 %copy-done.1 = f32[2,256,256]{2,1,0:T(8,128)S(1)} copy-done((f32[2,256,256]{2,1,0:T(8,128)S(1)}, f32[2,256,256]{2,1,0:T(8,128)}, u32[]{:S(2)}) %copy-start.1) | copy-done | bytes 524312
  9.1 0.7 pack.2
  9.8 0.4 collective-permute-start
  10.1 0.9 collective-permute-start.1
  11.0 0.0 collective-permute-done.4.refs_1_
  11.0 1.6 %collective-permute-start.2 = (f32[2,2,80,128]{3,2,1,0:T(8,128)S(1)}, f32[2,2,80,128]{3,2,1,0:T(8,128)S(1)}, u32[]{:S(2)}, u32[]{:S(2)}) collective-permute-start(f32[2,2,80,128]{3,2,1,0:T(8,128)S(1)} %get-tuple-element.52), channel_id=1, source_target_pairs={{0,3},{1,0},{2,1},{3,2},{4,7},{5,4},{6,5},{7,6},{8,11},{9,8},{10,9... | collective-permute-start | bytes 491528 | tf_op jit(solution)/shard_map/ppermute | solution.py:401
  12.6 1.4 %collective-permute-done.5.refs_2_ = f32[2,2,80,128]{3,2,1,0:T(8,128)S(1)} collective-permute-done((f32[2,2,80,128]{3,2,1,0:T(8,128)S(1)}, f32[2,2,80,128]{3,2,1,0:T(8,128)S(1)}, u32[]{:S(2)}, u32[]{:S(2)}) %collective-permute-start.5) | collective-permute-done | bytes 163872 | tf_op jit(solution)/shard_map/ppermute | solution.py:401
  14.1 0.0 collective-permute-done.6.refs_3_
  14.1 0.1 join.3.own
  14.1 2.8 %collective-permute-start.8 = (f32[8,2,80,128]{3,2,1,0:T(8,128)S(1)}, f32[8,2,80,128]{3,2,1,0:T(8,128)S(1)}, u32[]{:S(2)}, u32[]{:S(2)}) collective-permute-start(f32[8,2,80,128]{3,2,1,0:T(8,128)S(1)} %join.3.own), channel_id=1, source_target_pairs={{0,4},{4,0},{1,5},{5,1},{2,6},{6,2},{3,7},{7,3},{8,12},{12,8},{9,1... | collective-permute-start | bytes 1966088 | tf_op jit(solution)/shard_map/ppermute | solution.py:424
  17.0 1.4 %collective-permute-done.refs_1_ = f32[2,2,80,128]{3,2,1,0:T(8,128)S(1)} collective-permute-done((f32[2,2,80,128]{3,2,1,0:T(8,128)S(1)}, f32[2,2,80,128]{3,2,1,0:T(8,128)S(1)}, u32[]{:S(2)}, u32[]{:S(2)}) %collective-permute-start) | collective-permute-done | bytes 163872 | tf_op jit(solution)/shard_map/ppermute | solution.py:401
  18.4 2.7 %collective-permute-done.1.refs_2_ = f32[2,2,80,128]{3,2,1,0:T(8,128)S(1)} collective-permute-done((f32[2,2,80,128]{3,2,1,0:T(8,128)S(1)}, f32[2,2,80,128]{3,2,1,0:T(8,128)S(1)}, u32[]{:S(2)}, u32[]{:S(2)}) %collective-permute-start.1) | collective-permute-done | bytes 163872 | tf_op jit(solution)/shard_map/ppermute | solution.py:401
  21.1 0.0 collective-permute-done.2.refs_3_
  21.1 0.1 join.2.own
  21.2 1.7 %collective-permute-start.9 = (f32[8,2,80,128]{3,2,1,0:T(8,128)S(1)}, f32[8,2,80,128]{3,2,1,0:T(8,128)S(1)}, u32[]{:S(2)}, u32[]{:S(2)}) collective-permute-start(f32[8,2,80,128]{3,2,1,0:T(8,128)S(1)} %join.2.own), channel_id=1, source_target_pairs={{0,4},{4,0},{1,5},{5,1},{2,6},{6,2},{3,7},{7,3},{8,12},{12,8},{9,1... | collective-permute-start | bytes 1966088 | tf_op jit(solution)/shard_map/ppermute | solution.py:424
  22.8 3.3 %collective-permute-start.7 = (f32[8,2,80,128]{3,2,1,0:T(8,128)S(1)}, f32[8,2,80,128]{3,2,1,0:T(8,128)S(1)}, u32[]{:S(2)}, u32[]{:S(2)}) collective-permute-start(f32[8,2,80,128]{3,2,1,0:T(8,128)S(1)} %join.3.own), channel_id=1, source_target_pairs={{8,4},{16,12},{24,20},{32,28},{40,36},{48,44},{56,52},{64,60},{72,... | collective-permute-start | bytes 1966088 | tf_op jit(solution)/shard_map/ppermute | solution.py:425
  26.2 2.4 %collective-permute-start.3 = (f32[7,2,80,128]{3,2,1,0:T(8,128)S(1)}, f32[7,2,80,128]{3,2,1,0:T(8,128)S(1)}, u32[]{:S(2)}, u32[]{:S(2)}) collective-permute-start(f32[7,2,80,128]{3,2,1,0:T(8,128)S(1)} %slice.4), channel_id=1, source_target_pairs={{8,4},{16,12},{24,20},{32,28},{40,36},{48,44},{56,52},{64,60},{72,... | collective-permute-start | bytes 1720328 | tf_op jit(solution)/shard_map/ppermute | solution.py:425
  28.6 0.0 collective-permute-done.8.side
  28.6 2.2 %near_chain.2 = (f32[24,2,96,128]{3,2,1,0:T(8,128)S(1)}, f32[22,2,96,128]{3,2,1,0:T(8,128)S(1)}, f32[20,2,96,128]{3,2,1,0:T(8,128)S(1)}, f32[18,2,96,128]{3,2,1,...) custom-call(f32[8,2,80,128]{3,2,1,0:T(8,128)S(1)} %join.3.own, ...), custom_call_target="tpu_custom_call" | custom-call | flops 40000000 | tf_op jit(solution)/shard_map/near_chain/pallas_call | solution.py:436
  30.8 0.0 collective-permute-done.9.side
  30.8 1.5 %near_chain.3 = (f32[24,2,96,128]{3,2,1,0:T(8,128)S(1)}, f32[20,2,96,128]{3,2,1,0:T(8,128)S(1)}, f32[18,2,96,128]{3,2,1,0:T(8,128)S(1)}, f32[16,2,96,128]{3,2,1,...) custom-call(f32[8,2,80,128]{3,2,1,0:T(8,128)S(1)} %join.2.own, ...), custom_call_target="tpu_custom_call" | custom-call | flops 40000000 | tf_op jit(solution)/shard_map/near_chain/pallas_call | solution.py:436
  32.4 2.4 %collective-permute-done.7.across = f32[8,2,80,128]{3,2,1,0:T(8,128)S(1)} collective-permute-done((f32[8,2,80,128]{3,2,1,0:T(8,128)S(1)}, f32[8,2,80,128]{3,2,1,0:T(8,128)S(1)}, u32[]{:S(2)}, u32[]{:S(2)}) %collective-permute-start.7) | collective-permute-done | bytes 655392 | tf_op jit(solution)/shard_map/ppermute | solution.py:425
  34.7 2.6 %far_direction.1 = (f32[24,2,96,128]{3,2,1,0:T(8,128)S(1)}, f32[22,2,96,128]{3,2,1,0:T(8,128)S(1)}, f32[20,2,96,128]{3,2,1,0:T(8,128)S(1)}, f32[18,2,96,128]{3,2...) custom-call(f32[8,2,80,128]{3,2,1,0:T(8,128)S(1)} %collective-permut, ...), custom_call_target="tpu_custom_call", output_to_operand_aliasing={{0}: (1, {}), {1}: (2, {}), {2}: (3, {}), {3}: (4, {}), {4}... | custom-call | flops 40000000 | tf_op jit(solution)/shard_map/far_direction/pallas_call | solution.py:450
  37.4 3.5 %collective-permute-done.3.across = f32[7,2,80,128]{3,2,1,0:T(8,128)S(1)} collective-permute-done((f32[7,2,80,128]{3,2,1,0:T(8,128)S(1)}, f32[7,2,80,128]{3,2,1,0:T(8,128)S(1)}, u32[]{:S(2)}, u32[]{:S(2)}) %collective-permute-start.3) | collective-permute-done | bytes 573472 | tf_op jit(solution)/shard_map/ppermute | solution.py:425
  40.9 2.9 %far_residual.1 = (f32[24,2,96,128]{3,2,1,0:T(8,128)S(1)}, f32[20,2,96,128]{3,2,1,0:T(8,128)S(1)}, f32[18,2,96,128]{3,2,1,0:T(8,128)S(1)}, f32[16,2,96,128]{3,2,...) custom-call(f32[7,2,80,128]{3,2,1,0:T(8,128)S(1)} %collective-permut, ...), custom_call_target="tpu_custom_call", output_to_operand_aliasing={{0}: (11, {}), {1}: (12, {}), {2}: (13, {}), {3}: (14, {}),... | custom-call | flops 40000000 | tf_op jit(solution)/shard_map/far_residual/pallas_call | solution.py:462
  43.7 0.1 broadcast_in_dim.9
  43.8 27.5 %all_to_all.5 = f32[256,1,128]{2,1,0:T(1,128)S(1)} all-to-all(f32[256,1,128]{2,1,0:T(1,128)S(1)} %broadcast_in_dim.9), channel_id=1, replica_groups=mesh['zz'=32,'c'=2,'x'=4] {'zz','c','x'}, dimensions={0} | all-to-all | bytes 262144 | tf_op jit(solution)/shard_map/all_to_all | solution.py:475
  71.3 3.8 %combine.4 = (f32[3,2,64,256]{3,2,1,0:T(8,128)S(1)}, f32[3,24,128]{2,1,0:T(8,128)S(1)}) custom-call(f32[256,128]{1,0:T(8,128)S(1)} %bitcast.2, f32[24,2,96,128]{3,2,1,0:T(8,128)S(1)} %get-tuple-element.66.refs_0_, f32[22,2,96,128]{3,2,1,0:T(8,128)S(1)} %get-tuple-element.67.refs_1_, f32[20,2,96,128]{3,2,1,0:T(8,128)S(1)} %get-tuple-element.68.refs_2_, ...), custom_call_target="tpu_custom_call" | custom-call | flops 40000000 | tf_op jit(solution)/shard_map/combine/pallas_call | solution.py:481
  75.1 1.1 %combine.7 = f32[3,2,64,256]{3,2,1,0:T(8,128)S(1)} custom-call(f32[3,24,128]{2,1,0:T(8,128)S(1)} %get-tuple-element.93.coefs, f32[24,2,96,128]{3,2,1,0:T(8,128)S(1)} %get-tuple-element.66.refs_0_, f32[22,2,96,128]{3,2,1,0:T(8,128)S(1)} %get-tuple-element.67.refs_1_, f32[20,2,96,128]{3,2,1,0:T(8,128)S(1)} %get-tuple-element.68.refs_2_, ...), custom_call_target="tpu_custom_call" | custom-call | flops 10000000 | tf_op jit(solution)/shard_map/combine/pallas_call | solution.py:492
  76.2 1.1 %combine.6 = f32[3,2,64,256]{3,2,1,0:T(8,128)S(1)} custom-call(f32[3,24,128]{2,1,0:T(8,128)S(1)} %get-tuple-element.93.coefs, f32[24,2,96,128]{3,2,1,0:T(8,128)S(1)} %get-tuple-element.66.refs_0_, f32[22,2,96,128]{3,2,1,0:T(8,128)S(1)} %get-tuple-element.67.refs_1_, f32[20,2,96,128]{3,2,1,0:T(8,128)S(1)} %get-tuple-element.68.refs_2_, ...), custom_call_target="tpu_custom_call" | custom-call | flops 10000000 | tf_op jit(solution)/shard_map/combine/pallas_call | solution.py:492
  77.3 0.8 collective-permute-start.12
  78.1 0.7 collective-permute-start.10
  78.8 0.0 copy-start.2
  78.8 0.8 collective-permute-start.11
  79.6 1.1 %combine.5.refs_0_ = f32[3,2,64,256]{3,2,1,0:T(8,128)S(1)} custom-call(f32[3,24,128]{2,1,0:T(8,128)S(1)} %get-tuple-element.93.coefs, f32[24,2,96,128]{3,2,1,0:T(8,128)S(1)} %get-tuple-element.66.refs_0_, f32[22,2,96,128]{3,2,1,0:T(8,128)S(1)} %get-tuple-element.67.refs_1_, f32[20,2,96,128]{3,2,1,0:T(8,128)S(1)} %get-tuple-element.68.refs_2_, ...), custom_call_target="tpu_custom_call" | custom-call | flops 10000000 | tf_op jit(solution)/shard_map/combine/pallas_call | solution.py:492
  80.7 6.4 %collective-permute-done.12.refs_3_ = f32[3,2,64,256]{3,2,1,0:T(8,128)S(1)} collective-permute-done((f32[3,2,64,256]{3,2,1,0:T(8,128)S(1)}, f32[3,2,64,256]{3,2,1,0:T(8,128)S(1)}, u32[]{:S(2)}, u32[]{:S(2)}) %collective-permute-start.12) | collective-permute-done | bytes 393248 | tf_op jit(solution)/shard_map/ppermute | solution.py:401
  87.1 3.0 %collective-permute-done.10.refs_1_ = f32[3,2,64,256]{3,2,1,0:T(8,128)S(1)} collective-permute-done((f32[3,2,64,256]{3,2,1,0:T(8,128)S(1)}, f32[3,2,64,256]{3,2,1,0:T(8,128)S(1)}, u32[]{:S(2)}, u32[]{:S(2)}) %collective-permute-start.10) | collective-permute-done | bytes 393248 | tf_op jit(solution)/shard_map/ppermute | solution.py:401
  90.0 6.3 %collective-permute-done.11.refs_2_ = f32[3,2,64,256]{3,2,1,0:T(8,128)S(1)} collective-permute-done((f32[3,2,64,256]{3,2,1,0:T(8,128)S(1)}, f32[3,2,64,256]{3,2,1,0:T(8,128)S(1)}, u32[]{:S(2)}, u32[]{:S(2)}) %collective-permute-start.11) | collective-permute-done | bytes 393248 | tf_op jit(solution)/shard_map/ppermute | solution.py:401
  96.3 0.0 copy-done.2
  96.3 1.2 %finish.1 = (f32[2,256,256]{2,1,0:T(8,128)}, f32[2,256,256]{2,1,0:T(8,128)}, f32[2,256,256]{2,1,0:T(8,128)}) custom-call(f32[2,256,256]{2,1,0:T(8,128)S(1)} %copy-done.2, f32[3,2,64,256]{3,2,1,0:T(8,128)S(1)} %combine.5.refs_0_, f32[3,2,64,256]{3,2,1,0:T(8,128)S(1)} %collective-permute-done.10.refs_1_, ...), custom_call_target="tpu_custom_call" | custom-call | tf_op jit(solution)/shard_map/finish/pallas_call | solution.py:507
  (1 shorter events, 0.0 us)
Async XLA Ops:
  0.6 1.0 %copy-start = (f32[2,256,256]{2,1,0:T(8,128)S(1)}, f32[2,256,256]{2,1,0:T(8,128)}, u32[]{:S(2)}) copy-start(f32[2,256,256]{2,1,0:T(8,128)} %source.3) | copy-start | bytes 1572868
  2.3 8.7 %collective-permute-start.4 = (f32[2,2,80,128]{3,2,1,0:T(8,128)S(1)}, f32[2,2,80,128]{3,2,1,0:T(8,128)S(1)}, u32[]{:S(2)}, u32[]{:S(2)}) collective-permute-start(f32[2,2,80,128]{3,2,1,0:T(8,128)S(1)} %get-tuple-element.54), channel_id=1, source_target_pairs={{0,1},{1,2},{2,3},{3,0},{4,5},{5,6},{6,7},{7,4},{8,9},{9,10},{10,1... | collective-permute-start | bytes 491528 | tf_op jit(solution)/shard_map/ppermute | solution.py:401
  4.4 9.6 %collective-permute-start.5 = (f32[2,2,80,128]{3,2,1,0:T(8,128)S(1)}, f32[2,2,80,128]{3,2,1,0:T(8,128)S(1)}, u32[]{:S(2)}, u32[]{:S(2)}) collective-permute-start(f32[2,2,80,128]{3,2,1,0:T(8,128)S(1)} %get-tuple-element.55), channel_id=1, source_target_pairs={{0,2},{1,3},{2,0},{3,1},{4,6},{5,7},{6,4},{7,5},{8,10},{9,11},{10,... | collective-permute-start | bytes 491528 | tf_op jit(solution)/shard_map/ppermute | solution.py:401
  6.9 7.2 %collective-permute-start.6 = (f32[2,2,80,128]{3,2,1,0:T(8,128)S(1)}, f32[2,2,80,128]{3,2,1,0:T(8,128)S(1)}, u32[]{:S(2)}, u32[]{:S(2)}) collective-permute-start(f32[2,2,80,128]{3,2,1,0:T(8,128)S(1)} %get-tuple-element.56), channel_id=1, source_target_pairs={{0,3},{1,0},{2,1},{3,2},{4,7},{5,4},{6,5},{7,6},{8,11},{9,8},{10,9... | collective-permute-start | bytes 491528 | tf_op jit(solution)/shard_map/ppermute | solution.py:401
  8.0 1.0 %copy-start.1 = (f32[2,256,256]{2,1,0:T(8,128)S(1)}, f32[2,256,256]{2,1,0:T(8,128)}, u32[]{:S(2)}) copy-start(f32[2,256,256]{2,1,0:T(8,128)} %source.2) | copy-start | bytes 1572868
  9.8 8.7 %collective-permute-start = (f32[2,2,80,128]{3,2,1,0:T(8,128)S(1)}, f32[2,2,80,128]{3,2,1,0:T(8,128)S(1)}, u32[]{:S(2)}, u32[]{:S(2)}) collective-permute-start(f32[2,2,80,128]{3,2,1,0:T(8,128)S(1)} %get-tuple-element.50), channel_id=1, source_target_pairs={{0,1},{1,2},{2,3},{3,0},{4,5},{5,6},{6,7},{7,4},{8,9},{9,10},{10,1... | collective-permute-start | bytes 491528 | tf_op jit(solution)/shard_map/ppermute | solution.py:401
  10.1 10.9 %collective-permute-start.1 = (f32[2,2,80,128]{3,2,1,0:T(8,128)S(1)}, f32[2,2,80,128]{3,2,1,0:T(8,128)S(1)}, u32[]{:S(2)}, u32[]{:S(2)}) collective-permute-start(f32[2,2,80,128]{3,2,1,0:T(8,128)S(1)} %get-tuple-element.51), channel_id=1, source_target_pairs={{0,2},{1,3},{2,0},{3,1},{4,6},{5,7},{6,4},{7,5},{8,10},{9,11},{10,... | collective-permute-start | bytes 491528 | tf_op jit(solution)/shard_map/ppermute | solution.py:401
  11.0 10.1 %collective-permute-start.2 = (f32[2,2,80,128]{3,2,1,0:T(8,128)S(1)}, f32[2,2,80,128]{3,2,1,0:T(8,128)S(1)}, u32[]{:S(2)}, u32[]{:S(2)}) collective-permute-start(f32[2,2,80,128]{3,2,1,0:T(8,128)S(1)} %get-tuple-element.52), channel_id=1, source_target_pairs={{0,3},{1,0},{2,1},{3,2},{4,7},{5,4},{6,5},{7,6},{8,11},{9,8},{10,9... | collective-permute-start | bytes 491528 | tf_op jit(solution)/shard_map/ppermute | solution.py:401
  14.1 14.5 %collective-permute-start.8 = (f32[8,2,80,128]{3,2,1,0:T(8,128)S(1)}, f32[8,2,80,128]{3,2,1,0:T(8,128)S(1)}, u32[]{:S(2)}, u32[]{:S(2)}) collective-permute-start(f32[8,2,80,128]{3,2,1,0:T(8,128)S(1)} %join.3.own), channel_id=1, source_target_pairs={{0,4},{4,0},{1,5},{5,1},{2,6},{6,2},{3,7},{7,3},{8,12},{12,8},{9,1... | collective-permute-start | bytes 1966088 | tf_op jit(solution)/shard_map/ppermute | solution.py:424
  21.2 9.7 %collective-permute-start.9 = (f32[8,2,80,128]{3,2,1,0:T(8,128)S(1)}, f32[8,2,80,128]{3,2,1,0:T(8,128)S(1)}, u32[]{:S(2)}, u32[]{:S(2)}) collective-permute-start(f32[8,2,80,128]{3,2,1,0:T(8,128)S(1)} %join.2.own), channel_id=1, source_target_pairs={{0,4},{4,0},{1,5},{5,1},{2,6},{6,2},{3,7},{7,3},{8,12},{12,8},{9,1... | collective-permute-start | bytes 1966088 | tf_op jit(solution)/shard_map/ppermute | solution.py:424
  22.8 11.9 %collective-permute-start.7 = (f32[8,2,80,128]{3,2,1,0:T(8,128)S(1)}, f32[8,2,80,128]{3,2,1,0:T(8,128)S(1)}, u32[]{:S(2)}, u32[]{:S(2)}) collective-permute-start(f32[8,2,80,128]{3,2,1,0:T(8,128)S(1)} %join.3.own), channel_id=1, source_target_pairs={{8,4},{16,12},{24,20},{32,28},{40,36},{48,44},{56,52},{64,60},{72,... | collective-permute-start | bytes 1966088 | tf_op jit(solution)/shard_map/ppermute | solution.py:425
  26.2 14.6 %collective-permute-start.3 = (f32[7,2,80,128]{3,2,1,0:T(8,128)S(1)}, f32[7,2,80,128]{3,2,1,0:T(8,128)S(1)}, u32[]{:S(2)}, u32[]{:S(2)}) collective-permute-start(f32[7,2,80,128]{3,2,1,0:T(8,128)S(1)} %slice.4), channel_id=1, source_target_pairs={{8,4},{16,12},{24,20},{32,28},{40,36},{48,44},{56,52},{64,60},{72,... | collective-permute-start | bytes 1720328 | tf_op jit(solution)/shard_map/ppermute | solution.py:425
  77.3 9.8 %collective-permute-start.12 = (f32[3,2,64,256]{3,2,1,0:T(8,128)S(1)}, f32[3,2,64,256]{3,2,1,0:T(8,128)S(1)}, u32[]{:S(2)}, u32[]{:S(2)}) collective-permute-start(f32[3,2,64,256]{3,2,1,0:T(8,128)S(1)} %combine.7), channel_id=1, source_target_pairs={{0,3},{1,0},{2,1},{3,2},{4,7},{5,4},{6,5},{7,6},{8,11},{9,8},{10,9... | collective-permute-start | bytes 1179656 | tf_op jit(solution)/shard_map/ppermute | solution.py:401
  78.1 11.9 %collective-permute-start.10 = (f32[3,2,64,256]{3,2,1,0:T(8,128)S(1)}, f32[3,2,64,256]{3,2,1,0:T(8,128)S(1)}, u32[]{:S(2)}, u32[]{:S(2)}) collective-permute-start(f32[3,2,64,256]{3,2,1,0:T(8,128)S(1)} %combine.6), channel_id=1, source_target_pairs={{0,1},{1,2},{2,3},{3,0},{4,5},{5,6},{6,7},{7,4},{8,9},{9,10},{10,1... | collective-permute-start | bytes 1179656 | tf_op jit(solution)/shard_map/ppermute | solution.py:401
  78.8 17.4 %copy-start.2 = (f32[2,256,256]{2,1,0:T(8,128)S(1)}, f32[2,256,256]{2,1,0:T(8,128)}, u32[]{:S(2)}) copy-start(f32[2,256,256]{2,1,0:T(8,128)} %solution.1) | copy-start | bytes 1572868
  78.8 17.4 %collective-permute-start.11 = (f32[3,2,64,256]{3,2,1,0:T(8,128)S(1)}, f32[3,2,64,256]{3,2,1,0:T(8,128)S(1)}, u32[]{:S(2)}, u32[]{:S(2)}) collective-permute-start(f32[3,2,64,256]{3,2,1,0:T(8,128)S(1)} %get-tuple-element.94), channel_id=1, source_target_pairs={{0,2},{1,3},{2,0},{3,1},{4,6},{5,7},{6,4},{7,5},{8,10},{9,11},{10,... | collective-permute-start | bytes 1179656 | tf_op jit(solution)/shard_map/ppermute | solution.py:401
where the time goes:
time: 98.2 us; the launch traced here: 97.7 us
  blocking collectives  27.5 us (28%)
  waiting for transfers between devices  27 us (27%)
  starting transfers between devices  21.2 us (22%)
  Pallas kernels  18.9 us (19%)
  local copies, waits for them, and re-layouts  2.19 us (2%)
    all_to_all x1, blocking collectives, on_device(): lax.all_to_all(jnp.broadcast_to(sums[None], (devices, 1, 128)), ALL, 0, 0...  27.5 us
    ppermute x9, waiting for transfers between devices, ahead(): lax.ppermute(value, 'x', [(i, (i + k) % groups) for i in range(groups)])  21.1 us
    ppermute x9, starting transfers between devices, ahead(): lax.ppermute(value, 'x', [(i, (i + k) % groups) for i in range(groups)])  10.9 us
    ppermute x2, waiting for transfers between devices, spread(): across = lax.ppermute(own[:reach], ('zz', 'c'), near)  5.87 us
    ppermute x2, starting transfers between devices, spread(): across = lax.ppermute(own[:reach], ('zz', 'c'), near)  5.73 us
    ppermute x2, starting transfers between devices, spread(): side = lax.ppermute(own, 'c', [(0, 1), (1, 0)])  4.51 us
    pallas_call x1, Pallas kernels, on_device(): pl.pallas_call(functools.partial(first_combine_kernel, first), out_shape=...  3.8 us
    pallas_call x2, Pallas kernels, near_chain(): pl.pallas_call(functools.partial(near_kernel, steps), out_shape=chain_sha...  3.7 us
  transfers between devices with their start and end apart: 13, of which 8 were waited for; matrix products, arithmetic and copies ran while one was open for 0% of the time, Pallas kernels for 8%

commit v1 on v0

--- a/solution.py
+++ b/solution.py
@@ -44,22 +44,35 @@
 def parting(back):
     i = lax.broadcasted_iota(jnp.int32, (2 * HALF, 2 * HALF), 0 if back else 1)
     j = lax.broadcasted_iota(jnp.int32, (2 * HALF, 2 * HALF), 1 if back else 0)
-    return (j == jnp.where(i < HALF, 2 * i, 2 * (i - HALF) + 1)).astype(jnp.float32)
+    return (j == jnp.where(i < HALF, 2 * i, 2 * (i - HALF) + 1)).astype(jnp.bfloat16)
 
 
 def move_columns(value, matrix):
-    return jnp.dot(value, matrix, precision=lax.Precision.HIGHEST, preferred_element_type=jnp.float32)
+    total = None
+    for _ in range(3):
+        part = value.astype(jnp.bfloat16)
+        moved = jnp.dot(part, matrix, preferred_element_type=jnp.float32)
+        total = moved if total is None else total + moved
+        value = value - part.astype(jnp.float32)
+    return total
+
+
+def part_columns(source, out):
+    matrix = parting(False)
+    for plane in range(source.shape[0]):
+        parted = move_columns(source[plane], matrix)
+        for h in range(2):
+            out[plane, h] = parted[:, h * HALF : (h + 1) * HALF]
 
 
 def pack_kernel(source, *refs):
-    outs, hold = refs[:PIECES], refs[PIECES]
+    part_columns(source, refs[PIECES])
+    cut_kernel(refs[PIECES], *refs[:PIECES])
+
+
+def cut_kernel(planes, *outs):
     per, halves, rows, _ = outs[0].shape
-    keep, height = rows - 2 * HALO, source.shape[1]
-    matrix = parting(False)
-    for plane in range(per):
-        parted = move_columns(source[plane], matrix)
-        for h in range(halves):
-            hold[plane, h] = parted[:, h * HALF : (h + 1) * HALF]
+    keep, height = rows - 2 * HALO, planes.shape[2]
     for k in range(PIECES):
         g = piece_of(k)
         row = pl.multiple_of(g * keep, keep)
@@ -68,14 +81,15 @@
         has_below, has_above = (g != 0).astype(jnp.float32), (g != PIECES - 1).astype(jnp.float32)
         for plane in range(per):
             for h in range(halves):
-                outs[k][plane, h, :HALO] = hold[plane, h, pl.ds(below, HALO)] * has_below
-                outs[k][plane, h, pl.ds(HALO, keep)] = hold[plane, h, pl.ds(row, keep)]
-                outs[k][plane, h, rows - HALO :] = hold[plane, h, pl.ds(above, HALO)] * has_above
-
-
-def join_kernel(*refs):
+                outs[k][plane, h, :HALO] = planes[plane, h, pl.ds(below, HALO)] * has_below
+                outs[k][plane, h, pl.ds(HALO, keep)] = planes[plane, h, pl.ds(row, keep)]
+                outs[k][plane, h, rows - HALO :] = planes[plane, h, pl.ds(above, HALO)] * has_above
+
+
+def join_kernel(mirrored, *refs):
     out = refs[PIECES]
     core, _ = here()
+    core = 1 - core if mirrored else core
     per = refs[0].shape[0]
     for k in range(PIECES):
         plane = per * piece_of(PIECES - k)
@@ -298,7 +312,9 @@
     down, along = change(i, 0), change(j, 1)
 
     def quadratic(left_down, right_along):
-        return jnp.sum(left_down * (gram * right_along), keepdims=True)
+        total = left_down * (gram * right_along)
+        total = total[:8] + total[8:16] + total[16:]
+        return jnp.sum(jnp.sum(total, axis=0, keepdims=True), axis=1, keepdims=True)
 
     def unit(index, k):
         return (index == k).astype(jnp.float32)
@@ -400,30 +416,39 @@
     def ahead(value, k):
         return lax.ppermute(value, "x", [(i, (i + k) % groups) for i in range(groups)])
 
-    def spread(field, reach):
-        pieces = pl.pallas_call(
+    piece = jax.ShapeDtypeStruct((per, 2, rows, HALF), f32)
+
+    def pack(field, name):
+        keeps = [jax.ShapeDtypeStruct((per, 2, height, HALF), f32)] if name == "r" else []
+        scratch = [] if name == "r" else [pltpu.VMEM((per, 2, height, HALF), f32)]
+        return pl.pallas_call(
             pack_kernel,
-            out_shape=(jax.ShapeDtypeStruct((per, 2, rows, HALF), f32),) * groups,
+            out_shape=[piece] * groups + keeps,
             in_specs=[VMEM],
-            out_specs=(VMEM,) * groups,
-            scratch_shapes=[pltpu.VMEM((per, 2, height, HALF), f32)],
+            out_specs=[VMEM] * (groups + len(keeps)),
+            scratch_shapes=scratch,
             compiler_params=params(),
             name="pack",
         )(field)
+
+    def spread(pieces, mirrored=False):
         got = [pieces[0]]
         for k in range(1, groups):
             got.append(ahead(pieces[k], k))
-        own = pl.pallas_call(
-            join_kernel,
+        return pl.pallas_call(
+            functools.partial(join_kernel, mirrored),
             out_shape=jax.ShapeDtypeStruct((PLANES, 2, rows, HALF), f32),
             in_specs=[VMEM] * groups,
             out_specs=VMEM,
             compiler_params=params(1),
             name="join",
         )(*got)
-        side = lax.ppermute(own, "c", [(0, 1), (1, 0)])
-        across = lax.ppermute(own[:reach], ("zz", "c"), near)
-        return own, side, across
+
+    def beside(own):
+        return lax.ppermute(own, "c", [(0, 1), (1, 0)])
+
+    def beyond(value):
+        return lax.ppermute(value, ("zz", "c"), near)
 
     def chain_shapes(steps):
         return tuple(
@@ -444,8 +469,21 @@
             name="near_chain",
         )(own, side)
 
-    own_d, side_d, across_d = spread(direction, S)
-    own_r, side_r, across_r = spread(residual, S - 1)
+    own_d = spread(pack(direction, "d"))
+    side_d, across_d = beside(own_d), beyond(own_d)
+    *pieces_r, parted_r = pack(residual, "r")
+    far_r = beyond(parted_r)
+    own_r = spread(pieces_r)
+    side_r = beside(own_r)
+    pieces_f = pl.pallas_call(
+        cut_kernel,
+        out_shape=[piece] * groups,
+        in_specs=[VMEM],
+        out_specs=[VMEM] * groups,
+        compiler_params=params(1),
+        name="cut",
+    )(far_r)
+    across_r = spread(pieces_f, mirrored=True)
     chain_d = near_chain(S, own_d, side_d)
     *chain_d, parts = pl.pallas_call(
         far_direction_kernel,

time: 98.2 us -> 104 us (1.059)
  starting transfers between devices: 21.2 us -> 24.3 us
  waiting for transfers between devices: 27 us -> 29.5 us
  blocking collectives: 27.5 us -> 29.1 us
  Pallas kernels: 18.9 us -> 17.4 us
    ppermute x9 -> x12, waiting for transfers between devices: 21.1 us -> 29.5 us  [ahead(): lax.ppermute(value, 'x', [(i, (i + k) % groups) for i in range(groups)])]
    ppermute x4, waiting for transfers between devices: 5.87 us -> 0.01 us  [the longest x2 0.01 us: beyond(): return lax.ppermute(value, ('zz', 'c'), near)]
    ppermute x9 -> x12, starting transfers between devices: 10.9 us -> 14.7 us  [ahead(): lax.ppermute(value, 'x', [(i, (i + k) % groups) for i in range(groups)])]
    all_to_all x1, blocking collectives: 27.5 us -> 29.1 us  [on_device(): lax.all_to_all(jnp.broadcast_to(sums[None], (devices, 1, 128)), ALL, 0, 0...]
  transfers between devices with their start and end apart: 13 -> 16, of which waited for: 8 -> 10; matrix products, arithmetic and copies ran while one was open for 0% -> 0% of each run, Pallas kernels for 8% -> 5%
where the time goes in v1:
time: 104 us; the launch traced here: 103 us
  waiting for transfers between devices  29.5 us (28%)
  blocking collectives  29.1 us (28%)
  starting transfers between devices  24.3 us (23%)
  Pallas kernels  17.4 us (17%)
  local copies, waits for them, and re-layouts  2.15 us (2%)
    ppermute x12, waiting for transfers between devices, ahead(): lax.ppermute(value, 'x', [(i, (i + k) % groups) for i in range(groups)])  29.5 us
    all_to_all x1, blocking collectives, on_device(): lax.all_to_all(jnp.broadcast_to(sums[None], (devices, 1, 128)), ALL, 0, 0...  29.1 us
    ppermute x12, starting transfers between devices, ahead(): lax.ppermute(value, 'x', [(i, (i + k) % groups) for i in range(groups)])  14.7 us
    ppermute x2, starting transfers between devices, beyond(): return lax.ppermute(value, ('zz', 'c'), near)  9.19 us
    pallas_call x2, Pallas kernels, near_chain(): pl.pallas_call(functools.partial(near_kernel, steps), out_shape=chain_sha...  3.75 us
    pallas_call x1, Pallas kernels, on_device(): pl.pallas_call(functools.partial(first_combine_kernel, first), out_shape=...  3.1 us
    pallas_call x1, Pallas kernels, on_device(): pl.pallas_call(far_residual_kernel, out_shape=(*chain_shapes(S - 1), jax....  2.88 us
    pallas_call x3, Pallas kernels, on_device(): pl.pallas_call(functools.partial(combine_kernel, k), out_shape=mixed_shap...  2.7 us
  transfers between devices with their start and end apart: 16, of which 10 were waited for; matrix products, arithmetic and copies ran while one was open for 0% of the time, Pallas kernels for 5%

profile of v1, /device:TPU:1, one launch (start us, length us, event | category | flops | bytes accessed | tf_op | source)
XLA Modules:
  0.0 103.4 jit_solution(636521933044711828)
XLA Ops:
  0.6 0.0 copy-start
  0.6 1.0 copy-done
  1.7 0.4 pack.3
  2.1 2.1 %collective-permute-start.4 = (f32[2,2,80,128]{3,2,1,0:T(8,128)S(1)}, f32[2,2,80,128]{3,2,1,0:T(8,128)S(1)}, u32[]{:S(2)}, u32[]{:S(2)}) collective-permute-start(f32[2,2,80,128]{3,2,1,0:T(8,128)S(1)} %get-tuple-element.60), channel_id=1, source_target_pairs={{0,1},{1,2},{2,3},{3,0},{4,5},{5,6},{6,7},{7,4},{8,9},{9,10},{10,1... | collective-permute-start | bytes 491528 | tf_op jit(solution)/shard_map/ppermute | solution.py:417
  4.2 2.5 %collective-permute-start.5 = (f32[2,2,80,128]{3,2,1,0:T(8,128)S(1)}, f32[2,2,80,128]{3,2,1,0:T(8,128)S(1)}, u32[]{:S(2)}, u32[]{:S(2)}) collective-permute-start(f32[2,2,80,128]{3,2,1,0:T(8,128)S(1)} %get-tuple-element.61), channel_id=1, source_target_pairs={{0,2},{1,3},{2,0},{3,1},{4,6},{5,7},{6,4},{7,5},{8,10},{9,11},{10,... | collective-permute-start | bytes 491528 | tf_op jit(solution)/shard_map/ppermute | solution.py:417
  6.7 0.0 copy-start.1
  6.7 1.0 %copy-done.1 = f32[2,256,256]{2,1,0:T(8,128)S(1)} copy-done((f32[2,256,256]{2,1,0:T(8,128)S(1)}, f32[2,256,256]{2,1,0:T(8,128)}, u32[]{:S(2)}) %copy-start.1) | copy-done | bytes 524312
  7.7 0.4 pack.2
  8.1 4.7 %collective-permute-start = (f32[2,2,256,128]{3,2,1,0:T(8,128)S(1)}, f32[2,2,256,128]{3,2,1,0:T(8,128)S(1)}, u32[]{:S(2)}, u32[]{:S(2)}) collective-permute-start(f32[2,2,256,128]{3,2,1,0:T(8,128)S(1)} %get-tuple-element.54), channel_id=1, source_target_pairs={{8,4},{16,12},{24,20},{32,28},{40,36},{48,44},{56,52},{64,60},{72,... | collective-permute-start | bytes 1572872 | tf_op jit(solution)/shard_map/ppermute | solution.py:451
  12.8 1.2 %collective-permute-start.6 = (f32[2,2,80,128]{3,2,1,0:T(8,128)S(1)}, f32[2,2,80,128]{3,2,1,0:T(8,128)S(1)}, u32[]{:S(2)}, u32[]{:S(2)}) collective-permute-start(f32[2,2,80,128]{3,2,1,0:T(8,128)S(1)} %get-tuple-element.62), channel_id=1, source_target_pairs={{0,3},{1,0},{2,1},{3,2},{4,7},{5,4},{6,5},{7,6},{8,11},{9,8},{10,9... | collective-permute-start | bytes 491528 | tf_op jit(solution)/shard_map/ppermute | solution.py:417
  14.0 0.2 collective-permute-start.10
  14.2 0.0 collective-permute-done.4.refs_1_
  14.3 2.5 %collective-permute-start.11 = (f32[2,2,80,128]{3,2,1,0:T(8,128)S(1)}, f32[2,2,80,128]{3,2,1,0:T(8,128)S(1)}, u32[]{:S(2)}, u32[]{:S(2)}) collective-permute-start(f32[2,2,80,128]{3,2,1,0:T(8,128)S(1)} %get-tuple-element.85), channel_id=1, source_target_pairs={{0,3},{1,0},{2,1},{3,2},{4,7},{5,4},{6,5},{7,6},{8,11},{9,8},{10,9... | collective-permute-start | bytes 491528 | tf_op jit(solution)/shard_map/ppermute | solution.py:417
  16.7 0.0 collective-permute-done.5.refs_2_
  16.7 0.0 collective-permute-start.9
  16.7 2.3 %collective-permute-done.6.refs_3_ = f32[2,2,80,128]{3,2,1,0:T(8,128)S(1)} collective-permute-done((f32[2,2,80,128]{3,2,1,0:T(8,128)S(1)}, f32[2,2,80,128]{3,2,1,0:T(8,128)S(1)}, u32[]{:S(2)}, u32[]{:S(2)}) %collective-permute-start.6) | collective-permute-done | bytes 163872 | tf_op jit(solution)/shard_map/ppermute | solution.py:417
  19.1 0.1 join.4.own
  19.2 0.1 collective-permute-start.8
  19.3 2.2 %collective-permute-done.10.refs_2_ = f32[2,2,80,128]{3,2,1,0:T(8,128)S(1)} collective-permute-done((f32[2,2,80,128]{3,2,1,0:T(8,128)S(1)}, f32[2,2,80,128]{3,2,1,0:T(8,128)S(1)}, u32[]{:S(2)}, u32[]{:S(2)}) %collective-permute-start.10) | collective-permute-done | bytes 163872 | tf_op jit(solution)/shard_map/ppermute | solution.py:417
  21.4 2.4 %collective-permute-done.11.refs_3_ = f32[2,2,80,128]{3,2,1,0:T(8,128)S(1)} collective-permute-done((f32[2,2,80,128]{3,2,1,0:T(8,128)S(1)}, f32[2,2,80,128]{3,2,1,0:T(8,128)S(1)}, u32[]{:S(2)}, u32[]{:S(2)}) %collective-permute-start.11) | collective-permute-done | bytes 163872 | tf_op jit(solution)/shard_map/ppermute | solution.py:417
  23.8 0.1 collective-permute-done.9.refs_1_
  24.0 0.1 join.5.own
  24.0 0.3 collective-permute-start.12
  24.4 4.5 %collective-permute-start.7 = (f32[8,2,80,128]{3,2,1,0:T(8,128)S(1)}, f32[8,2,80,128]{3,2,1,0:T(8,128)S(1)}, u32[]{:S(2)}, u32[]{:S(2)}) collective-permute-start(f32[8,2,80,128]{3,2,1,0:T(8,128)S(1)} %join.4.own), channel_id=1, source_target_pairs={{8,4},{16,12},{24,20},{32,28},{40,36},{48,44},{56,52},{64,60},{72,... | collective-permute-start | bytes 1966088 | tf_op jit(solution)/shard_map/ppermute | solution.py:451
  28.9 0.0 collective-permute-done.planes
  28.9 0.1 cut.1
  29.0 0.1 collective-permute-start.1
  29.1 3.5 %collective-permute-start.2 = (f32[2,2,80,128]{3,2,1,0:T(8,128)S(1)}, f32[2,2,80,128]{3,2,1,0:T(8,128)S(1)}, u32[]{:S(2)}, u32[]{:S(2)}) collective-permute-start(f32[2,2,80,128]{3,2,1,0:T(8,128)S(1)} %get-tuple-element.57), channel_id=1, source_target_pairs={{0,2},{1,3},{2,0},{3,1},{4,6},{5,7},{6,4},{7,5},{8,10},{9,11},{10,... | collective-permute-start | bytes 491528 | tf_op jit(solution)/shard_map/ppermute | solution.py:417
  32.6 2.7 %collective-permute-done.1.refs_1_ = f32[2,2,80,128]{3,2,1,0:T(8,128)S(1)} collective-permute-done((f32[2,2,80,128]{3,2,1,0:T(8,128)S(1)}, f32[2,2,80,128]{3,2,1,0:T(8,128)S(1)}, u32[]{:S(2)}, u32[]{:S(2)}) %collective-permute-start.1) | collective-permute-done | bytes 163872 | tf_op jit(solution)/shard_map/ppermute | solution.py:417
  35.3 0.3 collective-permute-start.3
  35.6 1.5 %collective-permute-done.2.refs_2_ = f32[2,2,80,128]{3,2,1,0:T(8,128)S(1)} collective-permute-done((f32[2,2,80,128]{3,2,1,0:T(8,128)S(1)}, f32[2,2,80,128]{3,2,1,0:T(8,128)S(1)}, u32[]{:S(2)}, u32[]{:S(2)}) %collective-permute-start.2) | collective-permute-done | bytes 163872 | tf_op jit(solution)/shard_map/ppermute | solution.py:417
  37.1 2.4 %collective-permute-done.3.refs_3_ = f32[2,2,80,128]{3,2,1,0:T(8,128)S(1)} collective-permute-done((f32[2,2,80,128]{3,2,1,0:T(8,128)S(1)}, f32[2,2,80,128]{3,2,1,0:T(8,128)S(1)}, u32[]{:S(2)}, u32[]{:S(2)}) %collective-permute-start.3) | collective-permute-done | bytes 163872 | tf_op jit(solution)/shard_map/ppermute | solution.py:417
  39.5 0.1 join.3.across
  39.5 0.0 collective-permute-done.8.side
  39.6 2.2 %near_chain.2 = (f32[24,2,96,128]{3,2,1,0:T(8,128)S(1)}, f32[22,2,96,128]{3,2,1,0:T(8,128)S(1)}, f32[20,2,96,128]{3,2,1,0:T(8,128)S(1)}, f32[18,2,96,128]{3,2,1,...) custom-call(f32[8,2,80,128]{3,2,1,0:T(8,128)S(1)} %join.4.own, ...), custom_call_target="tpu_custom_call" | custom-call | flops 40000000 | tf_op jit(solution)/shard_map/near_chain/pallas_call | solution.py:461
  41.8 0.0 collective-permute-done.12.side
  41.8 1.6 %near_chain.3 = (f32[24,2,96,128]{3,2,1,0:T(8,128)S(1)}, f32[20,2,96,128]{3,2,1,0:T(8,128)S(1)}, f32[18,2,96,128]{3,2,1,0:T(8,128)S(1)}, f32[16,2,96,128]{3,2,1,...) custom-call(f32[8,2,80,128]{3,2,1,0:T(8,128)S(1)} %join.5.own, ...), custom_call_target="tpu_custom_call" | custom-call | flops 40000000 | tf_op jit(solution)/shard_map/near_chain/pallas_call | solution.py:461
  43.3 0.0 collective-permute-done.7.across
  43.3 2.7 %far_direction.1 = (f32[24,2,96,128]{3,2,1,0:T(8,128)S(1)}, f32[22,2,96,128]{3,2,1,0:T(8,128)S(1)}, f32[20,2,96,128]{3,2,1,0:T(8,128)S(1)}, f32[18,2,96,128]{3,2...) custom-call(f32[8,2,80,128]{3,2,1,0:T(8,128)S(1)} %collective-permut, ...), custom_call_target="tpu_custom_call", output_to_operand_aliasing={{0}: (1, {}), {1}: (2, {}), {2}: (3, {}), {3}: (4, {}), {4}... | custom-call | flops 40000000 | tf_op jit(solution)/shard_map/far_direction/pallas_call | solution.py:488
  46.0 2.9 %far_residual.1 = (f32[24,2,96,128]{3,2,1,0:T(8,128)S(1)}, f32[20,2,96,128]{3,2,1,0:T(8,128)S(1)}, f32[18,2,96,128]{3,2,1,0:T(8,128)S(1)}, f32[16,2,96,128]{3,2,...) custom-call(f32[8,2,80,128]{3,2,1,0:T(8,128)S(1)} %join.3.across, ...), custom_call_target="tpu_custom_call", output_to_operand_aliasing={{0}: (11, {}), {1}: (12, {}), {2}: (13, {}), {3}: (14, {}),... | custom-call | flops 40000000 | tf_op jit(solution)/shard_map/far_residual/pallas_call | solution.py:500
  48.9 0.1 broadcast_in_dim.9
  49.0 29.1 %all_to_all.5 = f32[256,1,128]{2,1,0:T(1,128)S(1)} all-to-all(f32[256,1,128]{2,1,0:T(1,128)S(1)} %broadcast_in_dim.9), channel_id=1, replica_groups=mesh['zz'=32,'c'=2,'x'=4] {'zz','c','x'}, dimensions={0} | all-to-all | bytes 262144 | tf_op jit(solution)/shard_map/all_to_all | solution.py:513
  78.1 3.1 %combine.4 = (f32[3,2,64,256]{3,2,1,0:T(8,128)S(1)}, f32[3,24,128]{2,1,0:T(8,128)S(1)}) custom-call(f32[256,128]{1,0:T(8,128)S(1)} %bitcast.2, f32[24,2,96,128]{3,2,1,0:T(8,128)S(1)} %get-tuple-element.72.refs_0_, f32[22,2,96,128]{3,2,1,0:T(8,128)S(1)} %get-tuple-element.73.refs_1_, f32[20,2,96,128]{3,2,1,0:T(8,128)S(1)} %get-tuple-element.74.refs_2_, ...), custom_call_target="tpu_custom_call" | custom-call | flops 40000000 | tf_op jit(solution)/shard_map/combine/pallas_call | solution.py:519
  81.2 0.9 combine.7
  82.1 0.9 combine.6
  83.1 0.8 collective-permute-start.15
  83.9 0.7 collective-permute-start.13
  84.6 0.0 copy-start.2
  84.6 0.8 collective-permute-start.14
  85.4 0.9 combine.5.refs_0_
  86.3 6.5 %collective-permute-done.15.refs_3_ = f32[3,2,64,256]{3,2,1,0:T(8,128)S(1)} collective-permute-done((f32[3,2,64,256]{3,2,1,0:T(8,128)S(1)}, f32[3,2,64,256]{3,2,1,0:T(8,128)S(1)}, u32[]{:S(2)}, u32[]{:S(2)}) %collective-permute-start.15) | collective-permute-done | bytes 393248 | tf_op jit(solution)/shard_map/ppermute | solution.py:417
  92.8 2.9 %collective-permute-done.13.refs_1_ = f32[3,2,64,256]{3,2,1,0:T(8,128)S(1)} collective-permute-done((f32[3,2,64,256]{3,2,1,0:T(8,128)S(1)}, f32[3,2,64,256]{3,2,1,0:T(8,128)S(1)}, u32[]{:S(2)}, u32[]{:S(2)}) %collective-permute-start.13) | collective-permute-done | bytes 393248 | tf_op jit(solution)/shard_map/ppermute | solution.py:417
  95.8 6.3 %collective-permute-done.14.refs_2_ = f32[3,2,64,256]{3,2,1,0:T(8,128)S(1)} collective-permute-done((f32[3,2,64,256]{3,2,1,0:T(8,128)S(1)}, f32[3,2,64,256]{3,2,1,0:T(8,128)S(1)}, u32[]{:S(2)}, u32[]{:S(2)}) %collective-permute-start.14) | collective-permute-done | bytes 393248 | tf_op jit(solution)/shard_map/ppermute | solution.py:417
  102.0 0.0 copy-done.2
  102.0 1.2 %finish.1 = (f32[2,256,256]{2,1,0:T(8,128)}, f32[2,256,256]{2,1,0:T(8,128)}, f32[2,256,256]{2,1,0:T(8,128)}) custom-call(f32[2,256,256]{2,1,0:T(8,128)S(1)} %copy-done.2, f32[3,2,64,256]{3,2,1,0:T(8,128)S(1)} %combine.5.refs_0_, f32[3,2,64,256]{3,2,1,0:T(8,128)S(1)} %collective-permute-done.13.refs_1_, ...), custom_call_target="tpu_custom_call" | custom-call | tf_op jit(solution)/shard_map/finish/pallas_call | solution.py:545
Async XLA Ops:
  0.6 1.0 %copy-start = (f32[2,256,256]{2,1,0:T(8,128)S(1)}, f32[2,256,256]{2,1,0:T(8,128)}, u32[]{:S(2)}) copy-start(f32[2,256,256]{2,1,0:T(8,128)} %source.3) | copy-start | bytes 1572868
  2.1 12.2 %collective-permute-start.4 = (f32[2,2,80,128]{3,2,1,0:T(8,128)S(1)}, f32[2,2,80,128]{3,2,1,0:T(8,128)S(1)}, u32[]{:S(2)}, u32[]{:S(2)}) collective-permute-start(f32[2,2,80,128]{3,2,1,0:T(8,128)S(1)} %get-tuple-element.60), channel_id=1, source_target_pairs={{0,1},{1,2},{2,3},{3,0},{4,5},{5,6},{6,7},{7,4},{8,9},{9,10},{10,1... | collective-permute-start | bytes 491528 | tf_op jit(solution)/shard_map/ppermute | solution.py:417
  4.2 12.5 %collective-permute-start.5 = (f32[2,2,80,128]{3,2,1,0:T(8,128)S(1)}, f32[2,2,80,128]{3,2,1,0:T(8,128)S(1)}, u32[]{:S(2)}, u32[]{:S(2)}) collective-permute-start(f32[2,2,80,128]{3,2,1,0:T(8,128)S(1)} %get-tuple-element.61), channel_id=1, source_target_pairs={{0,2},{1,3},{2,0},{3,1},{4,6},{5,7},{6,4},{7,5},{8,10},{9,11},{10,... | collective-permute-start | bytes 491528 | tf_op jit(solution)/shard_map/ppermute | solution.py:417
  6.7 1.0 %copy-start.1 = (f32[2,256,256]{2,1,0:T(8,128)S(1)}, f32[2,256,256]{2,1,0:T(8,128)}, u32[]{:S(2)}) copy-start(f32[2,256,256]{2,1,0:T(8,128)} %source.2) | copy-start | bytes 1572868
  8.1 20.8 %collective-permute-start = (f32[2,2,256,128]{3,2,1,0:T(8,128)S(1)}, f32[2,2,256,128]{3,2,1,0:T(8,128)S(1)}, u32[]{:S(2)}, u32[]{:S(2)}) collective-permute-start(f32[2,2,256,128]{3,2,1,0:T(8,128)S(1)} %get-tuple-element.54), channel_id=1, source_target_pairs={{8,4},{16,12},{24,20},{32,28},{40,36},{48,44},{56,52},{64,60},{72,... | collective-permute-start | bytes 1572872 | tf_op jit(solution)/shard_map/ppermute | solution.py:451
  12.8 6.3 %collective-permute-start.6 = (f32[2,2,80,128]{3,2,1,0:T(8,128)S(1)}, f32[2,2,80,128]{3,2,1,0:T(8,128)S(1)}, u32[]{:S(2)}, u32[]{:S(2)}) collective-permute-start(f32[2,2,80,128]{3,2,1,0:T(8,128)S(1)} %get-tuple-element.62), channel_id=1, source_target_pairs={{0,3},{1,0},{2,1},{3,2},{4,7},{5,4},{6,5},{7,6},{8,11},{9,8},{10,9... | collective-permute-start | bytes 491528 | tf_op jit(solution)/shard_map/ppermute | solution.py:417
  14.0 7.4 %collective-permute-start.10 = (f32[2,2,80,128]{3,2,1,0:T(8,128)S(1)}, f32[2,2,80,128]{3,2,1,0:T(8,128)S(1)}, u32[]{:S(2)}, u32[]{:S(2)}) collective-permute-start(f32[2,2,80,128]{3,2,1,0:T(8,128)S(1)} %get-tuple-element.84), channel_id=1, source_target_pairs={{0,2},{1,3},{2,0},{3,1},{4,6},{5,7},{6,4},{7,5},{8,10},{9,11},{10,... | collective-permute-start | bytes 491528 | tf_op jit(solution)/shard_map/ppermute | solution.py:417
  14.3 9.6 %collective-permute-start.11 = (f32[2,2,80,128]{3,2,1,0:T(8,128)S(1)}, f32[2,2,80,128]{3,2,1,0:T(8,128)S(1)}, u32[]{:S(2)}, u32[]{:S(2)}) collective-permute-start(f32[2,2,80,128]{3,2,1,0:T(8,128)S(1)} %get-tuple-element.85), channel_id=1, source_target_pairs={{0,3},{1,0},{2,1},{3,2},{4,7},{5,4},{6,5},{7,6},{8,11},{9,8},{10,9... | collective-permute-start | bytes 491528 | tf_op jit(solution)/shard_map/ppermute | solution.py:417
  16.7 7.2 %collective-permute-start.9 = (f32[2,2,80,128]{3,2,1,0:T(8,128)S(1)}, f32[2,2,80,128]{3,2,1,0:T(8,128)S(1)}, u32[]{:S(2)}, u32[]{:S(2)}) collective-permute-start(f32[2,2,80,128]{3,2,1,0:T(8,128)S(1)} %get-tuple-element.83), channel_id=1, source_target_pairs={{0,1},{1,2},{2,3},{3,0},{4,5},{5,6},{6,7},{7,4},{8,9},{9,10},{10,1... | collective-permute-start | bytes 491528 | tf_op jit(solution)/shard_map/ppermute | solution.py:417
  19.2 20.4 %collective-permute-start.8 = (f32[8,2,80,128]{3,2,1,0:T(8,128)S(1)}, f32[8,2,80,128]{3,2,1,0:T(8,128)S(1)}, u32[]{:S(2)}, u32[]{:S(2)}) collective-permute-start(f32[8,2,80,128]{3,2,1,0:T(8,128)S(1)} %join.4.own), channel_id=1, source_target_pairs={{0,4},{4,0},{1,5},{5,1},{2,6},{6,2},{3,7},{7,3},{8,12},{12,8},{9,1... | collective-permute-start | bytes 1966088 | tf_op jit(solution)/shard_map/ppermute | solution.py:448
  24.0 17.7 %collective-permute-start.12 = (f32[8,2,80,128]{3,2,1,0:T(8,128)S(1)}, f32[8,2,80,128]{3,2,1,0:T(8,128)S(1)}, u32[]{:S(2)}, u32[]{:S(2)}) collective-permute-start(f32[8,2,80,128]{3,2,1,0:T(8,128)S(1)} %join.5.own), channel_id=1, source_target_pairs={{0,4},{4,0},{1,5},{5,1},{2,6},{6,2},{3,7},{7,3},{8,12},{12,8},{9,1... | collective-permute-start | bytes 1966088 | tf_op jit(solution)/shard_map/ppermute | solution.py:448
  24.4 19.0 %collective-permute-start.7 = (f32[8,2,80,128]{3,2,1,0:T(8,128)S(1)}, f32[8,2,80,128]{3,2,1,0:T(8,128)S(1)}, u32[]{:S(2)}, u32[]{:S(2)}) collective-permute-start(f32[8,2,80,128]{3,2,1,0:T(8,128)S(1)} %join.4.own), channel_id=1, source_target_pairs={{8,4},{16,12},{24,20},{32,28},{40,36},{48,44},{56,52},{64,60},{72,... | collective-permute-start | bytes 1966088 | tf_op jit(solution)/shard_map/ppermute | solution.py:451
  29.0 6.3 %collective-permute-start.1 = (f32[2,2,80,128]{3,2,1,0:T(8,128)S(1)}, f32[2,2,80,128]{3,2,1,0:T(8,128)S(1)}, u32[]{:S(2)}, u32[]{:S(2)}) collective-permute-start(f32[2,2,80,128]{3,2,1,0:T(8,128)S(1)} %get-tuple-element.56), channel_id=1, source_target_pairs={{0,1},{1,2},{2,3},{3,0},{4,5},{5,6},{6,7},{7,4},{8,9},{9,10},{10,1... | collective-permute-start | bytes 491528 | tf_op jit(solution)/shard_map/ppermute | solution.py:417
  29.1 8.0 %collective-permute-start.2 = (f32[2,2,80,128]{3,2,1,0:T(8,128)S(1)}, f32[2,2,80,128]{3,2,1,0:T(8,128)S(1)}, u32[]{:S(2)}, u32[]{:S(2)}) collective-permute-start(f32[2,2,80,128]{3,2,1,0:T(8,128)S(1)} %get-tuple-element.57), channel_id=1, source_target_pairs={{0,2},{1,3},{2,0},{3,1},{4,6},{5,7},{6,4},{7,5},{8,10},{9,11},{10,... | collective-permute-start | bytes 491528 | tf_op jit(solution)/shard_map/ppermute | solution.py:417
  35.3 4.2 %collective-permute-start.3 = (f32[2,2,80,128]{3,2,1,0:T(8,128)S(1)}, f32[2,2,80,128]{3,2,1,0:T(8,128)S(1)}, u32[]{:S(2)}, u32[]{:S(2)}) collective-permute-start(f32[2,2,80,128]{3,2,1,0:T(8,128)S(1)} %get-tuple-element.58), channel_id=1, source_target_pairs={{0,3},{1,0},{2,1},{3,2},{4,7},{5,4},{6,5},{7,6},{8,11},{9,8},{10,9... | collective-permute-start | bytes 491528 | tf_op jit(solution)/shard_map/ppermute | solution.py:417
  83.1 9.8 %collective-permute-start.15 = (f32[3,2,64,256]{3,2,1,0:T(8,128)S(1)}, f32[3,2,64,256]{3,2,1,0:T(8,128)S(1)}, u32[]{:S(2)}, u32[]{:S(2)}) collective-permute-start(f32[3,2,64,256]{3,2,1,0:T(8,128)S(1)} %combine.7), channel_id=1, source_target_pairs={{0,3},{1,0},{2,1},{3,2},{4,7},{5,4},{6,5},{7,6},{8,11},{9,8},{10,9... | collective-permute-start | bytes 1179656 | tf_op jit(solution)/shard_map/ppermute | solution.py:417
  83.9 11.9 %collective-permute-start.13 = (f32[3,2,64,256]{3,2,1,0:T(8,128)S(1)}, f32[3,2,64,256]{3,2,1,0:T(8,128)S(1)}, u32[]{:S(2)}, u32[]{:S(2)}) collective-permute-start(f32[3,2,64,256]{3,2,1,0:T(8,128)S(1)} %combine.6), channel_id=1, source_target_pairs={{0,1},{1,2},{2,3},{3,0},{4,5},{5,6},{6,7},{7,4},{8,9},{9,10},{10,1... | collective-permute-start | bytes 1179656 | tf_op jit(solution)/shard_map/ppermute | solution.py:417
  84.6 17.4 %copy-start.2 = (f32[2,256,256]{2,1,0:T(8,128)S(1)}, f32[2,256,256]{2,1,0:T(8,128)}, u32[]{:S(2)}) copy-start(f32[2,256,256]{2,1,0:T(8,128)} %solution.1) | copy-start | bytes 1572868
  84.6 17.4 %collective-permute-start.14 = (f32[3,2,64,256]{3,2,1,0:T(8,128)S(1)}, f32[3,2,64,256]{3,2,1,0:T(8,128)S(1)}, u32[]{:S(2)}, u32[]{:S(2)}) collective-permute-start(f32[3,2,64,256]{3,2,1,0:T(8,128)S(1)} %get-tuple-element.104), channel_id=1, source_target_pairs={{0,2},{1,3},{2,0},{3,1},{4,6},{5,7},{6,4},{7,5},{8,10},{9,11},{10,... | collective-permute-start | bytes 1179656 | tf_op jit(solution)/shard_map/ppermute | solution.py:417

commit v2 on v1

--- a/solution.py
+++ b/solution.py
@@ -17,6 +17,8 @@
 PAD = 8
 HALF = 128
 GROUP = 4
+BLOCK = 16
+AHEAD = 4
 FIRST = -1.0 / 6.0
 NEXT = -1.0 / 3.0
 ALL = ("zz", "c", "x")
@@ -104,9 +106,8 @@
             chain[0][place, h, rows] = source[i, h]
 
 
-def run_groups(groups, chain, sideways, rows, steps):
+def run_groups(groups, chain, rows, steps):
     lows, _ = chain_plan(steps)
-    data = pl.ds(PAD, rows)
     core, x = here()
     zz = lax.axis_index("zz")
     last = lax.axis_size("zz") - 1
@@ -114,71 +115,53 @@
     low_x = (x != 0).astype(jnp.float32)
     high_x = (x != PIECES - 1).astype(jnp.float32)
     across_valid = 1.0 - alone.astype(jnp.float32)
-    lane = lax.broadcasted_iota(jnp.int32, (rows, HALF), 1)
+    lane = lax.broadcasted_iota(jnp.int32, (BLOCK, HALF), 1)
     at_low, at_high = lane == 0, lane == HALF - 1
-
-    def neighbours_y(power, plane):
-        source = chain[power - 1]
-        index = plane - lows[power - 1]
-        a, b = source[index, 0, data], source[index, 1, data]
-        first = b + jnp.where(at_low, 0.0, pltpu.roll(b, 1, 1))
-        second = a + jnp.where(at_high, 0.0, pltpu.roll(a, HALF - 1, 1))
-        return first, second
-
-    def value(power, plane, slot, across):
-        now, new = chain[power - 1], chain[power]
-        index = plane - lows[power - 1]
-        scale = FIRST if power == 1 else NEXT
-        if across:
-            scale = scale * across_valid
-        for h in range(2):
-            total = now[index - 1, h, data] + now[index + 1, h, data]
-            total = total + (now[index, h, pl.ds(PAD - 1, rows)] + now[index, h, pl.ds(PAD + 1, rows)])
-            total = total + sideways[slot, h]
-            parts = []
-            for a, b, weight in ((0, HALO, low_x), (HALO, rows - HALO, None), (rows - HALO, rows, high_x)):
-                parts.append(total[a:b] * (scale if weight is None else scale * weight))
-            result = jnp.concatenate(parts, axis=0)
-            if power > 1:
-                result = result - chain[power - 2][plane - lows[power - 2], h, data]
-            new[plane - lows[power], h, data] = result
-
-    def step(group, then):
-        power, plane, count = group
-        made = [(power, plane + u) for u in range(count)] if isinstance(plane, int) else []
-        ahead, late = [], []
-        if then:
-            for u in range(then[2]):
-                if (then[0] - 1, then[1] + u) in made:
-                    late.append(u)
+    blocks = rows // BLOCK
+    items = [(power, plane, count, block) for power, plane, count in groups for block in range(blocks)]
+    missing = {(power, plane + u, block) for power, plane, count, block in items for u in range(count)}
+
+    def read(power, plane, h, block, shift=0):
+        return chain[power][plane - lows[power], h, pl.ds(PAD + BLOCK * block + shift, BLOCK)]
+
+    def rotate(power, plane, count, block):
+        turned = []
+        for u in range(count):
+            a, b = (read(power - 1, plane + u, h, block) for h in range(2))
+            turned.append((pltpu.roll(b, 1, 1), pltpu.roll(a, HALF - 1, 1)))
+        return turned
+
+    def compute(power, plane, count, block, turned):
+        near = [[read(power - 1, plane + u, h, block) for h in range(2)] for u in range(-1, count + 1)]
+        for u in range(count):
+            scale = FIRST if power == 1 else NEXT
+            if plane + u < HALO:
+                scale = scale * across_valid
+            for h in range(2):
+                beside = near[u + 1][1 - h] + jnp.where(at_high if h else at_low, 0.0, turned[u][h])
+                total = near[u][h] + near[u + 2][h]
+                total = total + (read(power - 1, plane + u, h, block, -1) + read(power - 1, plane + u, h, block, 1))
+                total = total + beside
+                if block == 0:
+                    total = jnp.concatenate([total[:HALO] * (scale * low_x), total[HALO:] * scale], axis=0)
+                elif block == blocks - 1:
+                    total = jnp.concatenate([total[:-HALO] * scale, total[-HALO:] * (scale * high_x)], axis=0)
                 else:
-                    ahead.append((u, neighbours_y(then[0], then[1] + u)))
-        for u in range(count):
-            value(power, plane + u, u, isinstance(plane, int) and plane + u < HALO)
-        ahead += [(u, neighbours_y(then[0], then[1] + u)) for u in late]
-        for u, pair in ahead:
-            sideways[u, 0], sideways[u, 1] = pair
-
-    first = groups[0]
-    for u in range(first[2]):
-        sideways[u, 0], sideways[u, 1] = neighbours_y(first[0], first[1] + u)
-    at = 0
-    while at < len(groups):
-        power, plane, count = groups[at]
-        run = 0
-        while at + run + 1 < len(groups) and groups[at + run + 1] == (power, plane + GROUP * (run + 1), count) and count == GROUP:
-            run += 1
-        if run >= 2:
-
-            def body(g, _, power=power, plane=plane):
-                now = plane + GROUP * g
-                step((power, now, GROUP), (power, now + GROUP, GROUP))
-                return 0
-
-            lax.fori_loop(0, run, body, 0)
-            at += run
-        step(groups[at], groups[at + 1] if at + 1 < len(groups) else None)
-        at += 1
+                    total = total * scale
+                if power > 1:
+                    total = total - read(power - 2, plane + u, h, block)
+                chain[power][plane + u - lows[power], h, pl.ds(PAD + BLOCK * block, BLOCK)] = total
+            missing.discard((power, plane + u, block))
+
+    turned, pushed = {}, 0
+    for i, item in enumerate(items):
+        while pushed < min(len(items), i + 1 + AHEAD):
+            power, plane, count, block = items[pushed]
+            if any((power - 1, plane + u, block) in missing for u in range(count)):
+                break
+            turned[pushed] = rotate(*items[pushed])
+            pushed += 1
+        compute(*item, turned.pop(i))
 
 
 def near_groups(steps):
@@ -207,13 +190,14 @@
 
 
 def near_kernel(steps, own, side, *refs):
-    chain, sideways = refs[: steps + 1], refs[steps + 1]
+    chain = refs[: steps + 1]
     load_planes(chain, own, range(HALO, HALO + PLANES))
     load_planes(chain, side, range(TALL - 1, HALO + PLANES - 1, -1))
-    run_groups(near_groups(steps), chain, sideways, own.shape[2], steps)
+    run_groups(near_groups(steps), chain, own.shape[2], steps)
 
 
 def add_products(acc, chain, steps, other, keep):
+    _, _ = chain_plan(steps)
     rows = pl.ds(PAD + HALO, keep)
     acc[...] = jnp.zeros_like(acc)
 
@@ -251,10 +235,10 @@
 
 
 def far_direction_kernel(across, *refs):
-    chain, parts, sideways, acc = refs[S + 1 : 2 * S + 2], refs[2 * S + 2], refs[2 * S + 3], refs[2 * S + 4]
+    chain, parts, acc = refs[S + 1 : 2 * S + 2], refs[2 * S + 2], refs[2 * S + 3]
     rows = across.shape[2]
     load_planes(chain, across, range(HALO - 1, HALO - 1 - across.shape[0], -1))
-    run_groups(far_groups(S), chain, sideways, rows, S)
+    run_groups(far_groups(S), chain, rows, S)
     add_products(acc, chain, S, None, rows - 2 * HALO)
     parts[...] = jnp.zeros_like(parts)
     put_products(acc, parts, DD)
@@ -262,10 +246,10 @@
 
 def far_residual_kernel(across, *refs):
     other, parts_d, refs = refs[: S + 1], refs[S + 1], refs[S + 2 :]
-    chain, sums, sideways, acc, parts = refs[S : 2 * S], refs[2 * S], refs[2 * S + 1], refs[2 * S + 2], refs[2 * S + 3]
+    chain, sums, acc, parts = refs[S : 2 * S], refs[2 * S], refs[2 * S + 1], refs[2 * S + 2]
     rows = across.shape[2]
     load_planes(chain, across, range(HALO - 1, HALO - 1 - across.shape[0], -1))
-    run_groups(far_groups(S - 1), chain, sideways, rows, S - 1)
+    run_groups(far_groups(S - 1), chain, rows, S - 1)
     add_products(acc, chain, S - 1, other, rows - 2 * HALO)
     parts[...] = parts_d[...]
     put_products(acc, parts, RR)
@@ -455,15 +439,12 @@
             jax.ShapeDtypeStruct((end - low, 2, rows + 2 * PAD, HALF), f32) for low, end in zip(*chain_plan(steps))
         )
 
-    sideways = pltpu.VMEM((GROUP, 2, rows, HALF), f32)
-
     def near_chain(steps, own, side):
         return pl.pallas_call(
             functools.partial(near_kernel, steps),
             out_shape=chain_shapes(steps),
             in_specs=[VMEM] * 2,
             out_specs=(VMEM,) * (steps + 1),
-            scratch_shapes=[sideways],
             compiler_params=params(),
             cost_estimate=cost(4),
             name="near_chain",
@@ -490,7 +471,7 @@
         out_shape=(*chain_shapes(S), jax.ShapeDtypeStruct((128, 128), f32)),
         in_specs=[VMEM] * (S + 2),
         out_specs=(VMEM,) * (S + 2),
-        scratch_shapes=[sideways, pltpu.VMEM((2 * S + 1, 8, HALF), f32)],
+        scratch_shapes=[pltpu.VMEM((2 * S + 1, 8, HALF), f32)],
         input_output_aliases={1 + k: k for k in range(S + 1)},
         compiler_params=params(),
         cost_estimate=cost(4),
@@ -502,7 +483,7 @@
         out_shape=(*chain_shapes(S - 1), jax.ShapeDtypeStruct((1, 128), f32)),
         in_specs=[VMEM] * (2 * S + 3),
         out_specs=(VMEM,) * (S + 1),
-        scratch_shapes=[sideways, pltpu.VMEM((4 * S - 1, 8, HALF), f32), pltpu.VMEM((128, 128), f32)],
+        scratch_shapes=[pltpu.VMEM((4 * S - 1, 8, HALF), f32), pltpu.VMEM((128, 128), f32)],
         input_output_aliases={S + 3 + k: k for k in range(S)},
         compiler_params=params(),
         cost_estimate=cost(4),

time: 104 us -> 103 us (level)
  Pallas kernels: 17.4 us -> 16.1 us
  transfers between devices with their start and end apart: 16 -> 16, of which waited for: 10 -> 10; matrix products, arithmetic and copies ran while one was open for 0% -> 0% of each run, Pallas kernels for 5% -> 4%
where the time goes in v2:
time: 103 us; the launch traced here: 102 us
  waiting for transfers between devices  29.5 us (29%)
  blocking collectives  29.1 us (28%)
  starting transfers between devices  24.3 us (24%)
  Pallas kernels  16.1 us (16%)
  local copies, waits for them, and re-layouts  2.15 us (2%)
    ppermute x12, waiting for transfers between devices, ahead(): lax.ppermute(value, 'x', [(i, (i + k) % groups) for i in range(groups)])  29.5 us
    all_to_all x1, blocking collectives, on_device(): lax.all_to_all(jnp.broadcast_to(sums[None], (devices, 1, 128)), ALL, 0, 0...  29.1 us
    ppermute x12, starting transfers between devices, ahead(): lax.ppermute(value, 'x', [(i, (i + k) % groups) for i in range(groups)])  14.7 us
    ppermute x2, starting transfers between devices, beyond(): return lax.ppermute(value, ('zz', 'c'), near)  9.19 us
    pallas_call x1, Pallas kernels, on_device(): pl.pallas_call(functools.partial(first_combine_kernel, first), out_shape=...  3.11 us
    pallas_call x2, Pallas kernels, near_chain(): pl.pallas_call(functools.partial(near_kernel, steps), out_shape=chain_sha...  2.79 us
    pallas_call x1, Pallas kernels, on_device(): pl.pallas_call(far_residual_kernel, out_shape=(*chain_shapes(S - 1), jax....  2.76 us
    pallas_call x3, Pallas kernels, on_device(): pl.pallas_call(functools.partial(combine_kernel, k), out_shape=mixed_shap...  2.69 us
  transfers between devices with their start and end apart: 16, of which 10 were waited for; matrix products, arithmetic and copies ran while one was open for 0% of the time, Pallas kernels for 4%

profile of v2, /device:TPU:1, one launch (start us, length us, event | category | flops | bytes accessed | tf_op | source)
XLA Modules:
  0.0 102.1 jit_solution(18360759268509869072)
XLA Ops:
  0.6 0.0 copy-start
  0.6 1.0 %copy-done = f32[2,256,256]{2,1,0:T(8,128)S(1)} copy-done((f32[2,256,256]{2,1,0:T(8,128)S(1)}, f32[2,256,256]{2,1,0:T(8,128)}, u32[]{:S(2)}) %copy-start) | copy-done | bytes 524312
  1.7 0.4 pack.3
  2.1 2.1 %collective-permute-start.4 = (f32[2,2,80,128]{3,2,1,0:T(8,128)S(1)}, f32[2,2,80,128]{3,2,1,0:T(8,128)S(1)}, u32[]{:S(2)}, u32[]{:S(2)}) collective-permute-start(f32[2,2,80,128]{3,2,1,0:T(8,128)S(1)} %get-tuple-element.60), channel_id=1, source_target_pairs={{0,1},{1,2},{2,3},{3,0},{4,5},{5,6},{6,7},{7,4},{8,9},{9,10},{10,1... | collective-permute-start | bytes 491528 | tf_op jit(solution)/shard_map/ppermute | solution.py:401
  4.2 2.5 %collective-permute-start.5 = (f32[2,2,80,128]{3,2,1,0:T(8,128)S(1)}, f32[2,2,80,128]{3,2,1,0:T(8,128)S(1)}, u32[]{:S(2)}, u32[]{:S(2)}) collective-permute-start(f32[2,2,80,128]{3,2,1,0:T(8,128)S(1)} %get-tuple-element.61), channel_id=1, source_target_pairs={{0,2},{1,3},{2,0},{3,1},{4,6},{5,7},{6,4},{7,5},{8,10},{9,11},{10,... | collective-permute-start | bytes 491528 | tf_op jit(solution)/shard_map/ppermute | solution.py:401
  6.7 0.0 copy-start.1
  6.7 1.0 %copy-done.1 = f32[2,256,256]{2,1,0:T(8,128)S(1)} copy-done((f32[2,256,256]{2,1,0:T(8,128)S(1)}, f32[2,256,256]{2,1,0:T(8,128)}, u32[]{:S(2)}) %copy-start.1) | copy-done | bytes 524312
  7.7 0.4 pack.2
  8.1 4.7 %collective-permute-start = (f32[2,2,256,128]{3,2,1,0:T(8,128)S(1)}, f32[2,2,256,128]{3,2,1,0:T(8,128)S(1)}, u32[]{:S(2)}, u32[]{:S(2)}) collective-permute-start(f32[2,2,256,128]{3,2,1,0:T(8,128)S(1)} %get-tuple-element.54), channel_id=1, source_target_pairs={{8,4},{16,12},{24,20},{32,28},{40,36},{48,44},{56,52},{64,60},{72,... | collective-permute-start | bytes 1572872 | tf_op jit(solution)/shard_map/ppermute | solution.py:435
  12.8 1.2 %collective-permute-start.6 = (f32[2,2,80,128]{3,2,1,0:T(8,128)S(1)}, f32[2,2,80,128]{3,2,1,0:T(8,128)S(1)}, u32[]{:S(2)}, u32[]{:S(2)}) collective-permute-start(f32[2,2,80,128]{3,2,1,0:T(8,128)S(1)} %get-tuple-element.62), channel_id=1, source_target_pairs={{0,3},{1,0},{2,1},{3,2},{4,7},{5,4},{6,5},{7,6},{8,11},{9,8},{10,9... | collective-permute-start | bytes 491528 | tf_op jit(solution)/shard_map/ppermute | solution.py:401
  14.0 0.2 collective-permute-start.10
  14.2 0.0 collective-permute-done.4.refs_1_
  14.3 2.5 %collective-permute-start.11 = (f32[2,2,80,128]{3,2,1,0:T(8,128)S(1)}, f32[2,2,80,128]{3,2,1,0:T(8,128)S(1)}, u32[]{:S(2)}, u32[]{:S(2)}) collective-permute-start(f32[2,2,80,128]{3,2,1,0:T(8,128)S(1)} %get-tuple-element.85), channel_id=1, source_target_pairs={{0,3},{1,0},{2,1},{3,2},{4,7},{5,4},{6,5},{7,6},{8,11},{9,8},{10,9... | collective-permute-start | bytes 491528 | tf_op jit(solution)/shard_map/ppermute | solution.py:401
  16.7 0.0 collective-permute-done.5.refs_2_
  16.7 0.0 collective-permute-start.9
  16.7 2.3 %collective-permute-done.6.refs_3_ = f32[2,2,80,128]{3,2,1,0:T(8,128)S(1)} collective-permute-done((f32[2,2,80,128]{3,2,1,0:T(8,128)S(1)}, f32[2,2,80,128]{3,2,1,0:T(8,128)S(1)}, u32[]{:S(2)}, u32[]{:S(2)}) %collective-permute-start.6) | collective-permute-done | bytes 163872 | tf_op jit(solution)/shard_map/ppermute | solution.py:401
  19.1 0.1 join.4.own
  19.2 0.1 collective-permute-start.8
  19.3 2.2 %collective-permute-done.10.refs_2_ = f32[2,2,80,128]{3,2,1,0:T(8,128)S(1)} collective-permute-done((f32[2,2,80,128]{3,2,1,0:T(8,128)S(1)}, f32[2,2,80,128]{3,2,1,0:T(8,128)S(1)}, u32[]{:S(2)}, u32[]{:S(2)}) %collective-permute-start.10) | collective-permute-done | bytes 163872 | tf_op jit(solution)/shard_map/ppermute | solution.py:401
  21.4 2.4 %collective-permute-done.11.refs_3_ = f32[2,2,80,128]{3,2,1,0:T(8,128)S(1)} collective-permute-done((f32[2,2,80,128]{3,2,1,0:T(8,128)S(1)}, f32[2,2,80,128]{3,2,1,0:T(8,128)S(1)}, u32[]{:S(2)}, u32[]{:S(2)}) %collective-permute-start.11) | collective-permute-done | bytes 163872 | tf_op jit(solution)/shard_map/ppermute | solution.py:401
  23.8 0.1 collective-permute-done.9.refs_1_
  24.0 0.1 join.5.own
  24.0 0.3 collective-permute-start.12
  24.4 4.5 %collective-permute-start.7 = (f32[8,2,80,128]{3,2,1,0:T(8,128)S(1)}, f32[8,2,80,128]{3,2,1,0:T(8,128)S(1)}, u32[]{:S(2)}, u32[]{:S(2)}) collective-permute-start(f32[8,2,80,128]{3,2,1,0:T(8,128)S(1)} %join.4.own), channel_id=1, source_target_pairs={{8,4},{16,12},{24,20},{32,28},{40,36},{48,44},{56,52},{64,60},{72,... | collective-permute-start | bytes 1966088 | tf_op jit(solution)/shard_map/ppermute | solution.py:435
  28.9 0.0 collective-permute-done.planes
  28.9 0.1 cut.1
  29.0 0.1 collective-permute-start.1
  29.1 3.5 %collective-permute-start.2 = (f32[2,2,80,128]{3,2,1,0:T(8,128)S(1)}, f32[2,2,80,128]{3,2,1,0:T(8,128)S(1)}, u32[]{:S(2)}, u32[]{:S(2)}) collective-permute-start(f32[2,2,80,128]{3,2,1,0:T(8,128)S(1)} %get-tuple-element.57), channel_id=1, source_target_pairs={{0,2},{1,3},{2,0},{3,1},{4,6},{5,7},{6,4},{7,5},{8,10},{9,11},{10,... | collective-permute-start | bytes 491528 | tf_op jit(solution)/shard_map/ppermute | solution.py:401
  32.6 2.7 %collective-permute-done.1.refs_1_ = f32[2,2,80,128]{3,2,1,0:T(8,128)S(1)} collective-permute-done((f32[2,2,80,128]{3,2,1,0:T(8,128)S(1)}, f32[2,2,80,128]{3,2,1,0:T(8,128)S(1)}, u32[]{:S(2)}, u32[]{:S(2)}) %collective-permute-start.1) | collective-permute-done | bytes 163872 | tf_op jit(solution)/shard_map/ppermute | solution.py:401
  35.3 0.3 collective-permute-start.3
  35.6 1.5 %collective-permute-done.2.refs_2_ = f32[2,2,80,128]{3,2,1,0:T(8,128)S(1)} collective-permute-done((f32[2,2,80,128]{3,2,1,0:T(8,128)S(1)}, f32[2,2,80,128]{3,2,1,0:T(8,128)S(1)}, u32[]{:S(2)}, u32[]{:S(2)}) %collective-permute-start.2) | collective-permute-done | bytes 163872 | tf_op jit(solution)/shard_map/ppermute | solution.py:401
  37.1 2.4 %collective-permute-done.3.refs_3_ = f32[2,2,80,128]{3,2,1,0:T(8,128)S(1)} collective-permute-done((f32[2,2,80,128]{3,2,1,0:T(8,128)S(1)}, f32[2,2,80,128]{3,2,1,0:T(8,128)S(1)}, u32[]{:S(2)}, u32[]{:S(2)}) %collective-permute-start.3) | collective-permute-done | bytes 163872 | tf_op jit(solution)/shard_map/ppermute | solution.py:401
  39.5 0.1 join.3.across
  39.5 0.0 collective-permute-done.8.side
  39.6 1.4 %near_chain.2 = (f32[24,2,96,128]{3,2,1,0:T(8,128)S(1)}, f32[22,2,96,128]{3,2,1,0:T(8,128)S(1)}, f32[20,2,96,128]{3,2,1,0:T(8,128)S(1)}, f32[18,2,96,128]{3,2,1,...) custom-call(f32[8,2,80,128]{3,2,1,0:T(8,128)S(1)} %join.4.own, ...), custom_call_target="tpu_custom_call" | custom-call | flops 40000000 | tf_op jit(solution)/shard_map/near_chain/pallas_call | solution.py:443
  41.0 0.0 collective-permute-done.12.side
  41.0 1.4 %near_chain.3 = (f32[24,2,96,128]{3,2,1,0:T(8,128)S(1)}, f32[20,2,96,128]{3,2,1,0:T(8,128)S(1)}, f32[18,2,96,128]{3,2,1,0:T(8,128)S(1)}, f32[16,2,96,128]{3,2,1,...) custom-call(f32[8,2,80,128]{3,2,1,0:T(8,128)S(1)} %join.5.own, ...), custom_call_target="tpu_custom_call" | custom-call | flops 40000000 | tf_op jit(solution)/shard_map/near_chain/pallas_call | solution.py:443
  42.4 0.0 collective-permute-done.7.across
  42.4 2.4 %far_direction.1 = (f32[24,2,96,128]{3,2,1,0:T(8,128)S(1)}, f32[22,2,96,128]{3,2,1,0:T(8,128)S(1)}, f32[20,2,96,128]{3,2,1,0:T(8,128)S(1)}, f32[18,2,96,128]{3,2...) custom-call(f32[8,2,80,128]{3,2,1,0:T(8,128)S(1)} %collective-permut, ...), custom_call_target="tpu_custom_call", output_to_operand_aliasing={{0}: (1, {}), {1}: (2, {}), {2}: (3, {}), {3}: (4, {}), {4}... | custom-call | flops 40000000 | tf_op jit(solution)/shard_map/far_direction/pallas_call | solution.py:469
  44.8 2.8 %far_residual.1 = (f32[24,2,96,128]{3,2,1,0:T(8,128)S(1)}, f32[20,2,96,128]{3,2,1,0:T(8,128)S(1)}, f32[18,2,96,128]{3,2,1,0:T(8,128)S(1)}, f32[16,2,96,128]{3,2,...) custom-call(f32[8,2,80,128]{3,2,1,0:T(8,128)S(1)} %join.3.across, ...), custom_call_target="tpu_custom_call", output_to_operand_aliasing={{0}: (11, {}), {1}: (12, {}), {2}: (13, {}), {3}: (14, {}),... | custom-call | flops 40000000 | tf_op jit(solution)/shard_map/far_residual/pallas_call | solution.py:481
  47.6 0.1 broadcast_in_dim.9
  47.7 29.1 %all_to_all.5 = f32[256,1,128]{2,1,0:T(1,128)S(1)} all-to-all(f32[256,1,128]{2,1,0:T(1,128)S(1)} %broadcast_in_dim.9), channel_id=1, replica_groups=mesh['zz'=32,'c'=2,'x'=4] {'zz','c','x'}, dimensions={0} | all-to-all | bytes 262144 | tf_op jit(solution)/shard_map/all_to_all | solution.py:494
  76.8 3.1 %combine.4 = (f32[3,2,64,256]{3,2,1,0:T(8,128)S(1)}, f32[3,24,128]{2,1,0:T(8,128)S(1)}) custom-call(f32[256,128]{1,0:T(8,128)S(1)} %bitcast.2, f32[24,2,96,128]{3,2,1,0:T(8,128)S(1)} %get-tuple-element.72.refs_0_, f32[22,2,96,128]{3,2,1,0:T(8,128)S(1)} %get-tuple-element.73.refs_1_, f32[20,2,96,128]{3,2,1,0:T(8,128)S(1)} %get-tuple-element.74.refs_2_, ...), custom_call_target="tpu_custom_call" | custom-call | flops 40000000 | tf_op jit(solution)/shard_map/combine/pallas_call | solution.py:500
  79.9 0.9 combine.7
  80.8 0.9 combine.6
  81.8 0.8 collective-permute-start.15
  82.6 0.7 collective-permute-start.13
  83.3 0.0 copy-start.2
  83.3 0.8 collective-permute-start.14
  84.1 0.9 combine.5.refs_0_
  85.0 6.5 %collective-permute-done.15.refs_3_ = f32[3,2,64,256]{3,2,1,0:T(8,128)S(1)} collective-permute-done((f32[3,2,64,256]{3,2,1,0:T(8,128)S(1)}, f32[3,2,64,256]{3,2,1,0:T(8,128)S(1)}, u32[]{:S(2)}, u32[]{:S(2)}) %collective-permute-start.15) | collective-permute-done | bytes 393248 | tf_op jit(solution)/shard_map/ppermute | solution.py:401
  91.5 2.9 %collective-permute-done.13.refs_1_ = f32[3,2,64,256]{3,2,1,0:T(8,128)S(1)} collective-permute-done((f32[3,2,64,256]{3,2,1,0:T(8,128)S(1)}, f32[3,2,64,256]{3,2,1,0:T(8,128)S(1)}, u32[]{:S(2)}, u32[]{:S(2)}) %collective-permute-start.13) | collective-permute-done | bytes 393248 | tf_op jit(solution)/shard_map/ppermute | solution.py:401
  94.5 6.3 %collective-permute-done.14.refs_2_ = f32[3,2,64,256]{3,2,1,0:T(8,128)S(1)} collective-permute-done((f32[3,2,64,256]{3,2,1,0:T(8,128)S(1)}, f32[3,2,64,256]{3,2,1,0:T(8,128)S(1)}, u32[]{:S(2)}, u32[]{:S(2)}) %collective-permute-start.14) | collective-permute-done | bytes 393248 | tf_op jit(solution)/shard_map/ppermute | solution.py:401
  100.7 0.0 copy-done.2
  100.7 1.2 %finish.1 = (f32[2,256,256]{2,1,0:T(8,128)}, f32[2,256,256]{2,1,0:T(8,128)}, f32[2,256,256]{2,1,0:T(8,128)}) custom-call(f32[2,256,256]{2,1,0:T(8,128)S(1)} %copy-done.2, f32[3,2,64,256]{3,2,1,0:T(8,128)S(1)} %combine.5.refs_0_, f32[3,2,64,256]{3,2,1,0:T(8,128)S(1)} %collective-permute-done.13.refs_1_, ...), custom_call_target="tpu_custom_call" | custom-call | tf_op jit(solution)/shard_map/finish/pallas_call | solution.py:526
Async XLA Ops:
  0.6 1.0 %copy-start = (f32[2,256,256]{2,1,0:T(8,128)S(1)}, f32[2,256,256]{2,1,0:T(8,128)}, u32[]{:S(2)}) copy-start(f32[2,256,256]{2,1,0:T(8,128)} %source.3) | copy-start | bytes 1572868
  2.1 12.2 %collective-permute-start.4 = (f32[2,2,80,128]{3,2,1,0:T(8,128)S(1)}, f32[2,2,80,128]{3,2,1,0:T(8,128)S(1)}, u32[]{:S(2)}, u32[]{:S(2)}) collective-permute-start(f32[2,2,80,128]{3,2,1,0:T(8,128)S(1)} %get-tuple-element.60), channel_id=1, source_target_pairs={{0,1},{1,2},{2,3},{3,0},{4,5},{5,6},{6,7},{7,4},{8,9},{9,10},{10,1... | collective-permute-start | bytes 491528 | tf_op jit(solution)/shard_map/ppermute | solution.py:401
  4.2 12.5 %collective-permute-start.5 = (f32[2,2,80,128]{3,2,1,0:T(8,128)S(1)}, f32[2,2,80,128]{3,2,1,0:T(8,128)S(1)}, u32[]{:S(2)}, u32[]{:S(2)}) collective-permute-start(f32[2,2,80,128]{3,2,1,0:T(8,128)S(1)} %get-tuple-element.61), channel_id=1, source_target_pairs={{0,2},{1,3},{2,0},{3,1},{4,6},{5,7},{6,4},{7,5},{8,10},{9,11},{10,... | collective-permute-start | bytes 491528 | tf_op jit(solution)/shard_map/ppermute | solution.py:401
  6.7 1.0 %copy-start.1 = (f32[2,256,256]{2,1,0:T(8,128)S(1)}, f32[2,256,256]{2,1,0:T(8,128)}, u32[]{:S(2)}) copy-start(f32[2,256,256]{2,1,0:T(8,128)} %source.2) | copy-start | bytes 1572868
  8.1 20.8 %collective-permute-start = (f32[2,2,256,128]{3,2,1,0:T(8,128)S(1)}, f32[2,2,256,128]{3,2,1,0:T(8,128)S(1)}, u32[]{:S(2)}, u32[]{:S(2)}) collective-permute-start(f32[2,2,256,128]{3,2,1,0:T(8,128)S(1)} %get-tuple-element.54), channel_id=1, source_target_pairs={{8,4},{16,12},{24,20},{32,28},{40,36},{48,44},{56,52},{64,60},{72,... | collective-permute-start | bytes 1572872 | tf_op jit(solution)/shard_map/ppermute | solution.py:435
  12.8 6.3 %collective-permute-start.6 = (f32[2,2,80,128]{3,2,1,0:T(8,128)S(1)}, f32[2,2,80,128]{3,2,1,0:T(8,128)S(1)}, u32[]{:S(2)}, u32[]{:S(2)}) collective-permute-start(f32[2,2,80,128]{3,2,1,0:T(8,128)S(1)} %get-tuple-element.62), channel_id=1, source_target_pairs={{0,3},{1,0},{2,1},{3,2},{4,7},{5,4},{6,5},{7,6},{8,11},{9,8},{10,9... | collective-permute-start | bytes 491528 | tf_op jit(solution)/shard_map/ppermute | solution.py:401
  14.0 7.4 %collective-permute-start.10 = (f32[2,2,80,128]{3,2,1,0:T(8,128)S(1)}, f32[2,2,80,128]{3,2,1,0:T(8,128)S(1)}, u32[]{:S(2)}, u32[]{:S(2)}) collective-permute-start(f32[2,2,80,128]{3,2,1,0:T(8,128)S(1)} %get-tuple-element.84), channel_id=1, source_target_pairs={{0,2},{1,3},{2,0},{3,1},{4,6},{5,7},{6,4},{7,5},{8,10},{9,11},{10,... | collective-permute-start | bytes 491528 | tf_op jit(solution)/shard_map/ppermute | solution.py:401
  14.3 9.6 %collective-permute-start.11 = (f32[2,2,80,128]{3,2,1,0:T(8,128)S(1)}, f32[2,2,80,128]{3,2,1,0:T(8,128)S(1)}, u32[]{:S(2)}, u32[]{:S(2)}) collective-permute-start(f32[2,2,80,128]{3,2,1,0:T(8,128)S(1)} %get-tuple-element.85), channel_id=1, source_target_pairs={{0,3},{1,0},{2,1},{3,2},{4,7},{5,4},{6,5},{7,6},{8,11},{9,8},{10,9... | collective-permute-start | bytes 491528 | tf_op jit(solution)/shard_map/ppermute | solution.py:401
  16.7 7.2 %collective-permute-start.9 = (f32[2,2,80,128]{3,2,1,0:T(8,128)S(1)}, f32[2,2,80,128]{3,2,1,0:T(8,128)S(1)}, u32[]{:S(2)}, u32[]{:S(2)}) collective-permute-start(f32[2,2,80,128]{3,2,1,0:T(8,128)S(1)} %get-tuple-element.83), channel_id=1, source_target_pairs={{0,1},{1,2},{2,3},{3,0},{4,5},{5,6},{6,7},{7,4},{8,9},{9,10},{10,1... | collective-permute-start | bytes 491528 | tf_op jit(solution)/shard_map/ppermute | solution.py:401
  19.2 20.4 %collective-permute-start.8 = (f32[8,2,80,128]{3,2,1,0:T(8,128)S(1)}, f32[8,2,80,128]{3,2,1,0:T(8,128)S(1)}, u32[]{:S(2)}, u32[]{:S(2)}) collective-permute-start(f32[8,2,80,128]{3,2,1,0:T(8,128)S(1)} %join.4.own), channel_id=1, source_target_pairs={{0,4},{4,0},{1,5},{5,1},{2,6},{6,2},{3,7},{7,3},{8,12},{12,8},{9,1... | collective-permute-start | bytes 1966088 | tf_op jit(solution)/shard_map/ppermute | solution.py:432
  24.0 16.9 %collective-permute-start.12 = (f32[8,2,80,128]{3,2,1,0:T(8,128)S(1)}, f32[8,2,80,128]{3,2,1,0:T(8,128)S(1)}, u32[]{:S(2)}, u32[]{:S(2)}) collective-permute-start(f32[8,2,80,128]{3,2,1,0:T(8,128)S(1)} %join.5.own), channel_id=1, source_target_pairs={{0,4},{4,0},{1,5},{5,1},{2,6},{6,2},{3,7},{7,3},{8,12},{12,8},{9,1... | collective-permute-start | bytes 1966088 | tf_op jit(solution)/shard_map/ppermute | solution.py:432
  24.4 18.0 %collective-permute-start.7 = (f32[8,2,80,128]{3,2,1,0:T(8,128)S(1)}, f32[8,2,80,128]{3,2,1,0:T(8,128)S(1)}, u32[]{:S(2)}, u32[]{:S(2)}) collective-permute-start(f32[8,2,80,128]{3,2,1,0:T(8,128)S(1)} %join.4.own), channel_id=1, source_target_pairs={{8,4},{16,12},{24,20},{32,28},{40,36},{48,44},{56,52},{64,60},{72,... | collective-permute-start | bytes 1966088 | tf_op jit(solution)/shard_map/ppermute | solution.py:435
  29.0 6.3 %collective-permute-start.1 = (f32[2,2,80,128]{3,2,1,0:T(8,128)S(1)}, f32[2,2,80,128]{3,2,1,0:T(8,128)S(1)}, u32[]{:S(2)}, u32[]{:S(2)}) collective-permute-start(f32[2,2,80,128]{3,2,1,0:T(8,128)S(1)} %get-tuple-element.56), channel_id=1, source_target_pairs={{0,1},{1,2},{2,3},{3,0},{4,5},{5,6},{6,7},{7,4},{8,9},{9,10},{10,1... | collective-permute-start | bytes 491528 | tf_op jit(solution)/shard_map/ppermute | solution.py:401
  29.1 8.0 %collective-permute-start.2 = (f32[2,2,80,128]{3,2,1,0:T(8,128)S(1)}, f32[2,2,80,128]{3,2,1,0:T(8,128)S(1)}, u32[]{:S(2)}, u32[]{:S(2)}) collective-permute-start(f32[2,2,80,128]{3,2,1,0:T(8,128)S(1)} %get-tuple-element.57), channel_id=1, source_target_pairs={{0,2},{1,3},{2,0},{3,1},{4,6},{5,7},{6,4},{7,5},{8,10},{9,11},{10,... | collective-permute-start | bytes 491528 | tf_op jit(solution)/shard_map/ppermute | solution.py:401
  35.3 4.2 %collective-permute-start.3 = (f32[2,2,80,128]{3,2,1,0:T(8,128)S(1)}, f32[2,2,80,128]{3,2,1,0:T(8,128)S(1)}, u32[]{:S(2)}, u32[]{:S(2)}) collective-permute-start(f32[2,2,80,128]{3,2,1,0:T(8,128)S(1)} %get-tuple-element.58), channel_id=1, source_target_pairs={{0,3},{1,0},{2,1},{3,2},{4,7},{5,4},{6,5},{7,6},{8,11},{9,8},{10,9... | collective-permute-start | bytes 491528 | tf_op jit(solution)/shard_map/ppermute | solution.py:401
  81.8 9.8 %collective-permute-start.15 = (f32[3,2,64,256]{3,2,1,0:T(8,128)S(1)}, f32[3,2,64,256]{3,2,1,0:T(8,128)S(1)}, u32[]{:S(2)}, u32[]{:S(2)}) collective-permute-start(f32[3,2,64,256]{3,2,1,0:T(8,128)S(1)} %combine.7), channel_id=1, source_target_pairs={{0,3},{1,0},{2,1},{3,2},{4,7},{5,4},{6,5},{7,6},{8,11},{9,8},{10,9... | collective-permute-start | bytes 1179656 | tf_op jit(solution)/shard_map/ppermute | solution.py:401
  82.6 11.9 %collective-permute-start.13 = (f32[3,2,64,256]{3,2,1,0:T(8,128)S(1)}, f32[3,2,64,256]{3,2,1,0:T(8,128)S(1)}, u32[]{:S(2)}, u32[]{:S(2)}) collective-permute-start(f32[3,2,64,256]{3,2,1,0:T(8,128)S(1)} %combine.6), channel_id=1, source_target_pairs={{0,1},{1,2},{2,3},{3,0},{4,5},{5,6},{6,7},{7,4},{8,9},{9,10},{10,1... | collective-permute-start | bytes 1179656 | tf_op jit(solution)/shard_map/ppermute | solution.py:401
  83.3 17.4 %copy-start.2 = (f32[2,256,256]{2,1,0:T(8,128)S(1)}, f32[2,256,256]{2,1,0:T(8,128)}, u32[]{:S(2)}) copy-start(f32[2,256,256]{2,1,0:T(8,128)} %solution.1) | copy-start | bytes 1572868
  83.3 17.4 %collective-permute-start.14 = (f32[3,2,64,256]{3,2,1,0:T(8,128)S(1)}, f32[3,2,64,256]{3,2,1,0:T(8,128)S(1)}, u32[]{:S(2)}, u32[]{:S(2)}) collective-permute-start(f32[3,2,64,256]{3,2,1,0:T(8,128)S(1)} %get-tuple-element.104), channel_id=1, source_target_pairs={{0,2},{1,3},{2,0},{3,1},{4,6},{5,7},{6,4},{7,5},{8,10},{9,11},{10,... | collective-permute-start | bytes 1179656 | tf_op jit(solution)/shard_map/ppermute | solution.py:401

commit v3 on v2

--- a/solution.py
+++ b/solution.py
@@ -70,6 +70,23 @@
 def pack_kernel(source, *refs):
     part_columns(source, refs[PIECES])
     cut_kernel(refs[PIECES], *refs[:PIECES])
+
+
+def first_pack_kernel(direction, residual, *refs):
+    outs, fetched, stage, parted, sem = refs[:PIECES], *refs[PIECES:]
+    copies = [
+        pltpu.make_async_copy(source.at[plane], to.at[plane], sem.at[2 * field + plane])
+        for field, (source, to) in enumerate(((direction, stage), (residual, fetched)))
+        for plane in range(direction.shape[0])
+    ]
+    for copy in copies:
+        copy.start()
+    for copy in copies[:2]:
+        copy.wait()
+    part_columns(stage, parted)
+    cut_kernel(parted, *outs)
+    for copy in copies[2:]:
+        copy.wait()
 
 
 def cut_kernel(planes, *outs):
@@ -402,18 +419,29 @@
 
     piece = jax.ShapeDtypeStruct((per, 2, rows, HALF), f32)
 
-    def pack(field, name):
-        keeps = [jax.ShapeDtypeStruct((per, 2, height, HALF), f32)] if name == "r" else []
-        scratch = [] if name == "r" else [pltpu.VMEM((per, 2, height, HALF), f32)]
-        return pl.pallas_call(
-            pack_kernel,
-            out_shape=[piece] * groups + keeps,
-            in_specs=[VMEM],
-            out_specs=[VMEM] * (groups + len(keeps)),
-            scratch_shapes=scratch,
-            compiler_params=params(),
-            name="pack",
-        )(field)
+    parted = jax.ShapeDtypeStruct((per, 2, height, HALF), f32)
+    whole = jax.ShapeDtypeStruct((per, height, lanes), f32)
+    *pieces_d, fetched = pl.pallas_call(
+        first_pack_kernel,
+        out_shape=[piece] * groups + [whole],
+        in_specs=[HBM] * 2,
+        out_specs=[VMEM] * (groups + 1),
+        scratch_shapes=[
+            pltpu.VMEM(whole.shape, f32),
+            pltpu.VMEM(parted.shape, f32),
+            pltpu.SemaphoreType.DMA((2 * per,)),
+        ],
+        compiler_params=params(),
+        name="pack",
+    )(*(pltpu.with_memory_space_constraint(field, pltpu.HBM) for field in (direction, residual)))
+    *pieces_r, parted_r = pl.pallas_call(
+        pack_kernel,
+        out_shape=[piece] * groups + [parted],
+        in_specs=[VMEM],
+        out_specs=[VMEM] * (groups + 1),
+        compiler_params=params(),
+        name="pack",
+    )(fetched)
 
     def spread(pieces, mirrored=False):
         got = [pieces[0]]
@@ -450,9 +478,8 @@
             name="near_chain",
         )(own, side)
 
-    own_d = spread(pack(direction, "d"))
+    own_d = spread(pieces_d)
     side_d, across_d = beside(own_d), beyond(own_d)
-    *pieces_r, parted_r = pack(residual, "r")
     far_r = beyond(parted_r)
     own_r = spread(pieces_r)
     side_r = beside(own_r)
@@ -522,7 +549,6 @@
     for k in range(1, groups):
         back.append(ahead(mixed[k], k))
 
-    whole = jax.ShapeDtypeStruct((per, height, lanes), f32)
     return pl.pallas_call(
         finish_kernel,
         out_shape=(whole,) * 3,

time: 103 us -> 102 us (level)
  local copies, waits for them, and re-layouts: 2.15 us -> 0.08 us
    unnamed x6 -> x2, local copies, waits for them, and re-layouts: 2.08 us -> 0.01 us
    pallas_call x2, Pallas kernels: 0.83 us -> 1.9 us  [the longest x1 1.49 us: on_device(): pl.pallas_call(first_pack_kernel, out_shape=[piece] * groups + [whole], i...]
where the time goes in v3:
time: 102 us; the launch traced here: 101 us
  waiting for transfers between devices  29.8 us (29%)
  blocking collectives  29 us (28%)
  starting transfers between devices  24.1 us (24%)
  Pallas kernels  17.1 us (17%)
    ppermute x12, waiting for transfers between devices, ahead(): lax.ppermute(value, 'x', [(i, (i + k) % groups) for i in range(groups)])  29.8 us
    all_to_all x1, blocking collectives, on_device(): lax.all_to_all(jnp.broadcast_to(sums[None], (devices, 1, 128)), ALL, 0, 0...  29 us
    ppermute x12, starting transfers between devices, ahead(): lax.ppermute(value, 'x', [(i, (i + k) % groups) for i in range(groups)])  14.7 us
    ppermute x2, starting transfers between devices, beyond(): return lax.ppermute(value, ('zz', 'c'), near)  8.73 us
    pallas_call x1, Pallas kernels, on_device(): pl.pallas_call(functools.partial(first_combine_kernel, first), out_shape=...  3.1 us
    pallas_call x2, Pallas kernels, near_chain(): pl.pallas_call(functools.partial(near_kernel, steps), out_shape=chain_sha...  2.79 us
    pallas_call x1, Pallas kernels, on_device(): pl.pallas_call(far_residual_kernel, out_shape=(*chain_shapes(S - 1), jax....  2.76 us
    pallas_call x3, Pallas kernels, on_device(): pl.pallas_call(functools.partial(combine_kernel, k), out_shape=mixed_shap...  2.69 us
  transfers between devices with their start and end apart: 16, of which 10 were waited for; matrix products, arithmetic and copies ran while one was open for 0% of the time, Pallas kernels for 4%

profile of v3, /device:TPU:1, one launch (start us, length us, event | category | flops | bytes accessed | tf_op | source)
XLA Modules:
  0.0 101.1 jit_solution(8939986703918945955)
XLA Ops:
  0.6 1.5 %pack.2 = (f32[2,2,80,128]{3,2,1,0:T(8,128)S(1)}, f32[2,2,80,128]{3,2,1,0:T(8,128)S(1)}, f32[2,2,80,128]{3,2,1,0:T(8,128)S(1)}, f32[2,2,80,128]{3,2,1,0:T(8,128)S(1)}, f32[2,256,256]{2,1,0:T(8,128)S(1)}) custom-call(f32[2,256,256]{2,1,0:T(8,128)} %direction.1, f32[2,256,256]{2,1,0:T(8,128)} %residual.1), custom_call_target="tpu_custom_call" | custom-call | tf_op jit(solution)/shard_map/pack/pallas_call | solution.py:424
  2.1 2.1 %collective-permute-start.4 = (f32[2,2,80,128]{3,2,1,0:T(8,128)S(1)}, f32[2,2,80,128]{3,2,1,0:T(8,128)S(1)}, u32[]{:S(2)}, u32[]{:S(2)}) collective-permute-start(f32[2,2,80,128]{3,2,1,0:T(8,128)S(1)} %get-tuple-element.62), channel_id=1, source_target_pairs={{0,1},{1,2},{2,3},{3,0},{4,5},{5,6},{6,7},{7,4},{8,9},{9,10},{10,1... | collective-permute-start | bytes 491528 | tf_op jit(solution)/shard_map/ppermute | solution.py:418
  4.2 2.5 %collective-permute-start.5 = (f32[2,2,80,128]{3,2,1,0:T(8,128)S(1)}, f32[2,2,80,128]{3,2,1,0:T(8,128)S(1)}, u32[]{:S(2)}, u32[]{:S(2)}) collective-permute-start(f32[2,2,80,128]{3,2,1,0:T(8,128)S(1)} %get-tuple-element.63), channel_id=1, source_target_pairs={{0,2},{1,3},{2,0},{3,1},{4,6},{5,7},{6,4},{7,5},{8,10},{9,11},{10,... | collective-permute-start | bytes 491528 | tf_op jit(solution)/shard_map/ppermute | solution.py:418
  6.7 0.4 pack.3
  7.1 4.7 %collective-permute-start = (f32[2,2,256,128]{3,2,1,0:T(8,128)S(1)}, f32[2,2,256,128]{3,2,1,0:T(8,128)S(1)}, u32[]{:S(2)}, u32[]{:S(2)}) collective-permute-start(f32[2,2,256,128]{3,2,1,0:T(8,128)S(1)} %get-tuple-element.56), channel_id=1, source_target_pairs={{8,4},{16,12},{24,20},{32,28},{40,36},{48,44},{56,52},{64,60},{72,... | collective-permute-start | bytes 1572872 | tf_op jit(solution)/shard_map/ppermute | solution.py:463
  11.8 1.2 %collective-permute-start.6 = (f32[2,2,80,128]{3,2,1,0:T(8,128)S(1)}, f32[2,2,80,128]{3,2,1,0:T(8,128)S(1)}, u32[]{:S(2)}, u32[]{:S(2)}) collective-permute-start(f32[2,2,80,128]{3,2,1,0:T(8,128)S(1)} %get-tuple-element.64), channel_id=1, source_target_pairs={{0,3},{1,0},{2,1},{3,2},{4,7},{5,4},{6,5},{7,6},{8,11},{9,8},{10,9... | collective-permute-start | bytes 491528 | tf_op jit(solution)/shard_map/ppermute | solution.py:418
  13.0 0.2 collective-permute-start.10
  13.2 0.0 collective-permute-done.4.refs_1_
  13.2 2.5 %collective-permute-start.11 = (f32[2,2,80,128]{3,2,1,0:T(8,128)S(1)}, f32[2,2,80,128]{3,2,1,0:T(8,128)S(1)}, u32[]{:S(2)}, u32[]{:S(2)}) collective-permute-start(f32[2,2,80,128]{3,2,1,0:T(8,128)S(1)} %get-tuple-element.87), channel_id=1, source_target_pairs={{0,3},{1,0},{2,1},{3,2},{4,7},{5,4},{6,5},{7,6},{8,11},{9,8},{10,9... | collective-permute-start | bytes 491528 | tf_op jit(solution)/shard_map/ppermute | solution.py:418
  15.7 0.0 collective-permute-done.5.refs_2_
  15.7 0.0 collective-permute-start.9
  15.7 2.5 %collective-permute-done.6.refs_3_ = f32[2,2,80,128]{3,2,1,0:T(8,128)S(1)} collective-permute-done((f32[2,2,80,128]{3,2,1,0:T(8,128)S(1)}, f32[2,2,80,128]{3,2,1,0:T(8,128)S(1)}, u32[]{:S(2)}, u32[]{:S(2)}) %collective-permute-start.6) | collective-permute-done | bytes 163872 | tf_op jit(solution)/shard_map/ppermute | solution.py:418
  18.3 0.1 join.4.own
  18.3 0.1 collective-permute-start.8
  18.4 1.2 %collective-permute-done.10.refs_2_ = f32[2,2,80,128]{3,2,1,0:T(8,128)S(1)} collective-permute-done((f32[2,2,80,128]{3,2,1,0:T(8,128)S(1)}, f32[2,2,80,128]{3,2,1,0:T(8,128)S(1)}, u32[]{:S(2)}, u32[]{:S(2)}) %collective-permute-start.10) | collective-permute-done | bytes 163872 | tf_op jit(solution)/shard_map/ppermute | solution.py:418
  19.6 3.3 %collective-permute-done.11.refs_3_ = f32[2,2,80,128]{3,2,1,0:T(8,128)S(1)} collective-permute-done((f32[2,2,80,128]{3,2,1,0:T(8,128)S(1)}, f32[2,2,80,128]{3,2,1,0:T(8,128)S(1)}, u32[]{:S(2)}, u32[]{:S(2)}) %collective-permute-start.11) | collective-permute-done | bytes 163872 | tf_op jit(solution)/shard_map/ppermute | solution.py:418
  22.9 0.3 collective-permute-done.9.refs_1_
  23.2 0.1 join.5.own
  23.3 0.6 collective-permute-start.12
  23.8 4.1 %collective-permute-start.7 = (f32[8,2,80,128]{3,2,1,0:T(8,128)S(1)}, f32[8,2,80,128]{3,2,1,0:T(8,128)S(1)}, u32[]{:S(2)}, u32[]{:S(2)}) collective-permute-start(f32[8,2,80,128]{3,2,1,0:T(8,128)S(1)} %join.4.own), channel_id=1, source_target_pairs={{8,4},{16,12},{24,20},{32,28},{40,36},{48,44},{56,52},{64,60},{72,... | collective-permute-start | bytes 1966088 | tf_op jit(solution)/shard_map/ppermute | solution.py:463
  27.9 0.0 collective-permute-done.planes
  27.9 0.1 cut.1
  28.0 0.1 collective-permute-start.1
  28.1 3.5 %collective-permute-start.2 = (f32[2,2,80,128]{3,2,1,0:T(8,128)S(1)}, f32[2,2,80,128]{3,2,1,0:T(8,128)S(1)}, u32[]{:S(2)}, u32[]{:S(2)}) collective-permute-start(f32[2,2,80,128]{3,2,1,0:T(8,128)S(1)} %get-tuple-element.59), channel_id=1, source_target_pairs={{0,2},{1,3},{2,0},{3,1},{4,6},{5,7},{6,4},{7,5},{8,10},{9,11},{10,... | collective-permute-start | bytes 491528 | tf_op jit(solution)/shard_map/ppermute | solution.py:418
  31.6 2.9 %collective-permute-done.1.refs_1_ = f32[2,2,80,128]{3,2,1,0:T(8,128)S(1)} collective-permute-done((f32[2,2,80,128]{3,2,1,0:T(8,128)S(1)}, f32[2,2,80,128]{3,2,1,0:T(8,128)S(1)}, u32[]{:S(2)}, u32[]{:S(2)}) %collective-permute-start.1) | collective-permute-done | bytes 163872 | tf_op jit(solution)/shard_map/ppermute | solution.py:418
  34.4 0.3 collective-permute-start.3
  34.7 1.5 %collective-permute-done.2.refs_2_ = f32[2,2,80,128]{3,2,1,0:T(8,128)S(1)} collective-permute-done((f32[2,2,80,128]{3,2,1,0:T(8,128)S(1)}, f32[2,2,80,128]{3,2,1,0:T(8,128)S(1)}, u32[]{:S(2)}, u32[]{:S(2)}) %collective-permute-start.2) | collective-permute-done | bytes 163872 | tf_op jit(solution)/shard_map/ppermute | solution.py:418
  36.2 2.4 %collective-permute-done.3.refs_3_ = f32[2,2,80,128]{3,2,1,0:T(8,128)S(1)} collective-permute-done((f32[2,2,80,128]{3,2,1,0:T(8,128)S(1)}, f32[2,2,80,128]{3,2,1,0:T(8,128)S(1)}, u32[]{:S(2)}, u32[]{:S(2)}) %collective-permute-start.3) | collective-permute-done | bytes 163872 | tf_op jit(solution)/shard_map/ppermute | solution.py:418
  38.6 0.1 join.3.across
  38.6 0.0 collective-permute-done.8.side
  38.6 1.4 %near_chain.2 = (f32[24,2,96,128]{3,2,1,0:T(8,128)S(1)}, f32[22,2,96,128]{3,2,1,0:T(8,128)S(1)}, f32[20,2,96,128]{3,2,1,0:T(8,128)S(1)}, f32[18,2,96,128]{3,2,1,...) custom-call(f32[8,2,80,128]{3,2,1,0:T(8,128)S(1)} %join.4.own, ...), custom_call_target="tpu_custom_call" | custom-call | flops 40000000 | tf_op jit(solution)/shard_map/near_chain/pallas_call | solution.py:471
  40.0 0.0 collective-permute-done.12.side
  40.1 1.4 %near_chain.3 = (f32[24,2,96,128]{3,2,1,0:T(8,128)S(1)}, f32[20,2,96,128]{3,2,1,0:T(8,128)S(1)}, f32[18,2,96,128]{3,2,1,0:T(8,128)S(1)}, f32[16,2,96,128]{3,2,1,...) custom-call(f32[8,2,80,128]{3,2,1,0:T(8,128)S(1)} %join.5.own, ...), custom_call_target="tpu_custom_call" | custom-call | flops 40000000 | tf_op jit(solution)/shard_map/near_chain/pallas_call | solution.py:471
  41.5 0.0 collective-permute-done.7.across
  41.5 2.4 %far_direction.1 = (f32[24,2,96,128]{3,2,1,0:T(8,128)S(1)}, f32[22,2,96,128]{3,2,1,0:T(8,128)S(1)}, f32[20,2,96,128]{3,2,1,0:T(8,128)S(1)}, f32[18,2,96,128]{3,2...) custom-call(f32[8,2,80,128]{3,2,1,0:T(8,128)S(1)} %collective-permut, ...), custom_call_target="tpu_custom_call", output_to_operand_aliasing={{0}: (1, {}), {1}: (2, {}), {2}: (3, {}), {3}: (4, {}), {4}... | custom-call | flops 40000000 | tf_op jit(solution)/shard_map/far_direction/pallas_call | solution.py:496
  43.9 2.8 %far_residual.1 = (f32[24,2,96,128]{3,2,1,0:T(8,128)S(1)}, f32[20,2,96,128]{3,2,1,0:T(8,128)S(1)}, f32[18,2,96,128]{3,2,1,0:T(8,128)S(1)}, f32[16,2,96,128]{3,2,...) custom-call(f32[8,2,80,128]{3,2,1,0:T(8,128)S(1)} %join.3.across, ...), custom_call_target="tpu_custom_call", output_to_operand_aliasing={{0}: (11, {}), {1}: (12, {}), {2}: (13, {}), {3}: (14, {}),... | custom-call | flops 40000000 | tf_op jit(solution)/shard_map/far_residual/pallas_call | solution.py:508
  46.7 0.1 broadcast_in_dim.9
  46.8 29.0 %all_to_all.5 = f32[256,1,128]{2,1,0:T(1,128)S(1)} all-to-all(f32[256,1,128]{2,1,0:T(1,128)S(1)} %broadcast_in_dim.9), channel_id=1, replica_groups=mesh['zz'=32,'c'=2,'x'=4] {'zz','c','x'}, dimensions={0} | all-to-all | bytes 262144 | tf_op jit(solution)/shard_map/all_to_all | solution.py:521
  75.8 3.1 %combine.4 = (f32[3,2,64,256]{3,2,1,0:T(8,128)S(1)}, f32[3,24,128]{2,1,0:T(8,128)S(1)}) custom-call(f32[256,128]{1,0:T(8,128)S(1)} %bitcast.2, f32[24,2,96,128]{3,2,1,0:T(8,128)S(1)} %get-tuple-element.74.refs_0_, f32[22,2,96,128]{3,2,1,0:T(8,128)S(1)} %get-tuple-element.75.refs_1_, f32[20,2,96,128]{3,2,1,0:T(8,128)S(1)} %get-tuple-element.76.refs_2_, ...), custom_call_target="tpu_custom_call" | custom-call | flops 40000000 | tf_op jit(solution)/shard_map/combine/pallas_call | solution.py:527
  78.9 0.9 combine.7
  79.8 0.9 combine.6
  80.7 0.8 collective-permute-start.15
  81.5 0.7 collective-permute-start.13
  82.3 0.0 copy-start
  82.3 0.8 collective-permute-start.14
  83.1 0.9 combine.5.refs_0_
  84.0 6.5 %collective-permute-done.15.refs_3_ = f32[3,2,64,256]{3,2,1,0:T(8,128)S(1)} collective-permute-done((f32[3,2,64,256]{3,2,1,0:T(8,128)S(1)}, f32[3,2,64,256]{3,2,1,0:T(8,128)S(1)}, u32[]{:S(2)}, u32[]{:S(2)}) %collective-permute-start.15) | collective-permute-done | bytes 393248 | tf_op jit(solution)/shard_map/ppermute | solution.py:418
  90.5 3.0 %collective-permute-done.13.refs_1_ = f32[3,2,64,256]{3,2,1,0:T(8,128)S(1)} collective-permute-done((f32[3,2,64,256]{3,2,1,0:T(8,128)S(1)}, f32[3,2,64,256]{3,2,1,0:T(8,128)S(1)}, u32[]{:S(2)}, u32[]{:S(2)}) %collective-permute-start.13) | collective-permute-done | bytes 393248 | tf_op jit(solution)/shard_map/ppermute | solution.py:418
  93.5 6.2 %collective-permute-done.14.refs_2_ = f32[3,2,64,256]{3,2,1,0:T(8,128)S(1)} collective-permute-done((f32[3,2,64,256]{3,2,1,0:T(8,128)S(1)}, f32[3,2,64,256]{3,2,1,0:T(8,128)S(1)}, u32[]{:S(2)}, u32[]{:S(2)}) %collective-permute-start.14) | collective-permute-done | bytes 393248 | tf_op jit(solution)/shard_map/ppermute | solution.py:418
  99.7 0.0 copy-done
  99.7 1.2 %finish.1 = (f32[2,256,256]{2,1,0:T(8,128)}, f32[2,256,256]{2,1,0:T(8,128)}, f32[2,256,256]{2,1,0:T(8,128)}) custom-call(f32[2,256,256]{2,1,0:T(8,128)S(1)} %copy-done, f32[3,2,64,256]{3,2,1,0:T(8,128)S(1)} %combine.5.refs_0_, f32[3,2,64,256]{3,2,1,0:T(8,128)S(1)} %collective-permute-done.13.refs_1_, f32[3,2,64,256]{3,2,1,0:T(8,128)S(1)} %collective-permute-done.14.refs_2_, ...), custom_call_target="tpu_custom_call" | custom-call | tf_op jit(solution)/shard_map/finish/pallas_call | solution.py:552
Async XLA Ops:
  2.1 11.1 %collective-permute-start.4 = (f32[2,2,80,128]{3,2,1,0:T(8,128)S(1)}, f32[2,2,80,128]{3,2,1,0:T(8,128)S(1)}, u32[]{:S(2)}, u32[]{:S(2)}) collective-permute-start(f32[2,2,80,128]{3,2,1,0:T(8,128)S(1)} %get-tuple-element.62), channel_id=1, source_target_pairs={{0,1},{1,2},{2,3},{3,0},{4,5},{5,6},{6,7},{7,4},{8,9},{9,10},{10,1... | collective-permute-start | bytes 491528 | tf_op jit(solution)/shard_map/ppermute | solution.py:418
  4.2 11.5 %collective-permute-start.5 = (f32[2,2,80,128]{3,2,1,0:T(8,128)S(1)}, f32[2,2,80,128]{3,2,1,0:T(8,128)S(1)}, u32[]{:S(2)}, u32[]{:S(2)}) collective-permute-start(f32[2,2,80,128]{3,2,1,0:T(8,128)S(1)} %get-tuple-element.63), channel_id=1, source_target_pairs={{0,2},{1,3},{2,0},{3,1},{4,6},{5,7},{6,4},{7,5},{8,10},{9,11},{10,... | collective-permute-start | bytes 491528 | tf_op jit(solution)/shard_map/ppermute | solution.py:418
  7.1 20.8 %collective-permute-start = (f32[2,2,256,128]{3,2,1,0:T(8,128)S(1)}, f32[2,2,256,128]{3,2,1,0:T(8,128)S(1)}, u32[]{:S(2)}, u32[]{:S(2)}) collective-permute-start(f32[2,2,256,128]{3,2,1,0:T(8,128)S(1)} %get-tuple-element.56), channel_id=1, source_target_pairs={{8,4},{16,12},{24,20},{32,28},{40,36},{48,44},{56,52},{64,60},{72,... | collective-permute-start | bytes 1572872 | tf_op jit(solution)/shard_map/ppermute | solution.py:463
  11.8 6.5 %collective-permute-start.6 = (f32[2,2,80,128]{3,2,1,0:T(8,128)S(1)}, f32[2,2,80,128]{3,2,1,0:T(8,128)S(1)}, u32[]{:S(2)}, u32[]{:S(2)}) collective-permute-start(f32[2,2,80,128]{3,2,1,0:T(8,128)S(1)} %get-tuple-element.64), channel_id=1, source_target_pairs={{0,3},{1,0},{2,1},{3,2},{4,7},{5,4},{6,5},{7,6},{8,11},{9,8},{10,9... | collective-permute-start | bytes 491528 | tf_op jit(solution)/shard_map/ppermute | solution.py:418
  13.0 6.6 %collective-permute-start.10 = (f32[2,2,80,128]{3,2,1,0:T(8,128)S(1)}, f32[2,2,80,128]{3,2,1,0:T(8,128)S(1)}, u32[]{:S(2)}, u32[]{:S(2)}) collective-permute-start(f32[2,2,80,128]{3,2,1,0:T(8,128)S(1)} %get-tuple-element.86), channel_id=1, source_target_pairs={{0,2},{1,3},{2,0},{3,1},{4,6},{5,7},{6,4},{7,5},{8,10},{9,11},{10,... | collective-permute-start | bytes 491528 | tf_op jit(solution)/shard_map/ppermute | solution.py:418
  13.2 9.7 %collective-permute-start.11 = (f32[2,2,80,128]{3,2,1,0:T(8,128)S(1)}, f32[2,2,80,128]{3,2,1,0:T(8,128)S(1)}, u32[]{:S(2)}, u32[]{:S(2)}) collective-permute-start(f32[2,2,80,128]{3,2,1,0:T(8,128)S(1)} %get-tuple-element.87), channel_id=1, source_target_pairs={{0,3},{1,0},{2,1},{3,2},{4,7},{5,4},{6,5},{7,6},{8,11},{9,8},{10,9... | collective-permute-start | bytes 491528 | tf_op jit(solution)/shard_map/ppermute | solution.py:418
  15.7 7.5 %collective-permute-start.9 = (f32[2,2,80,128]{3,2,1,0:T(8,128)S(1)}, f32[2,2,80,128]{3,2,1,0:T(8,128)S(1)}, u32[]{:S(2)}, u32[]{:S(2)}) collective-permute-start(f32[2,2,80,128]{3,2,1,0:T(8,128)S(1)} %get-tuple-element.85), channel_id=1, source_target_pairs={{0,1},{1,2},{2,3},{3,0},{4,5},{5,6},{6,7},{7,4},{8,9},{9,10},{10,1... | collective-permute-start | bytes 491528 | tf_op jit(solution)/shard_map/ppermute | solution.py:418
  18.3 20.3 %collective-permute-start.8 = (f32[8,2,80,128]{3,2,1,0:T(8,128)S(1)}, f32[8,2,80,128]{3,2,1,0:T(8,128)S(1)}, u32[]{:S(2)}, u32[]{:S(2)}) collective-permute-start(f32[8,2,80,128]{3,2,1,0:T(8,128)S(1)} %join.4.own), channel_id=1, source_target_pairs={{0,4},{4,0},{1,5},{5,1},{2,6},{6,2},{3,7},{7,3},{8,12},{12,8},{9,1... | collective-permute-start | bytes 1966088 | tf_op jit(solution)/shard_map/ppermute | solution.py:460
  23.3 16.8 %collective-permute-start.12 = (f32[8,2,80,128]{3,2,1,0:T(8,128)S(1)}, f32[8,2,80,128]{3,2,1,0:T(8,128)S(1)}, u32[]{:S(2)}, u32[]{:S(2)}) collective-permute-start(f32[8,2,80,128]{3,2,1,0:T(8,128)S(1)} %join.5.own), channel_id=1, source_target_pairs={{0,4},{4,0},{1,5},{5,1},{2,6},{6,2},{3,7},{7,3},{8,12},{12,8},{9,1... | collective-permute-start | bytes 1966088 | tf_op jit(solution)/shard_map/ppermute | solution.py:460
  23.8 17.6 %collective-permute-start.7 = (f32[8,2,80,128]{3,2,1,0:T(8,128)S(1)}, f32[8,2,80,128]{3,2,1,0:T(8,128)S(1)}, u32[]{:S(2)}, u32[]{:S(2)}) collective-permute-start(f32[8,2,80,128]{3,2,1,0:T(8,128)S(1)} %join.4.own), channel_id=1, source_target_pairs={{8,4},{16,12},{24,20},{32,28},{40,36},{48,44},{56,52},{64,60},{72,... | collective-permute-start | bytes 1966088 | tf_op jit(solution)/shard_map/ppermute | solution.py:463
  28.0 6.4 %collective-permute-start.1 = (f32[2,2,80,128]{3,2,1,0:T(8,128)S(1)}, f32[2,2,80,128]{3,2,1,0:T(8,128)S(1)}, u32[]{:S(2)}, u32[]{:S(2)}) collective-permute-start(f32[2,2,80,128]{3,2,1,0:T(8,128)S(1)} %get-tuple-element.58), channel_id=1, source_target_pairs={{0,1},{1,2},{2,3},{3,0},{4,5},{5,6},{6,7},{7,4},{8,9},{9,10},{10,1... | collective-permute-start | bytes 491528 | tf_op jit(solution)/shard_map/ppermute | solution.py:418
  28.1 8.1 %collective-permute-start.2 = (f32[2,2,80,128]{3,2,1,0:T(8,128)S(1)}, f32[2,2,80,128]{3,2,1,0:T(8,128)S(1)}, u32[]{:S(2)}, u32[]{:S(2)}) collective-permute-start(f32[2,2,80,128]{3,2,1,0:T(8,128)S(1)} %get-tuple-element.59), channel_id=1, source_target_pairs={{0,2},{1,3},{2,0},{3,1},{4,6},{5,7},{6,4},{7,5},{8,10},{9,11},{10,... | collective-permute-start | bytes 491528 | tf_op jit(solution)/shard_map/ppermute | solution.py:418
  34.4 4.2 %collective-permute-start.3 = (f32[2,2,80,128]{3,2,1,0:T(8,128)S(1)}, f32[2,2,80,128]{3,2,1,0:T(8,128)S(1)}, u32[]{:S(2)}, u32[]{:S(2)}) collective-permute-start(f32[2,2,80,128]{3,2,1,0:T(8,128)S(1)} %get-tuple-element.60), channel_id=1, source_target_pairs={{0,3},{1,0},{2,1},{3,2},{4,7},{5,4},{6,5},{7,6},{8,11},{9,8},{10,9... | collective-permute-start | bytes 491528 | tf_op jit(solution)/shard_map/ppermute | solution.py:418
  80.7 9.8 %collective-permute-start.15 = (f32[3,2,64,256]{3,2,1,0:T(8,128)S(1)}, f32[3,2,64,256]{3,2,1,0:T(8,128)S(1)}, u32[]{:S(2)}, u32[]{:S(2)}) collective-permute-start(f32[3,2,64,256]{3,2,1,0:T(8,128)S(1)} %combine.7), channel_id=1, source_target_pairs={{0,3},{1,0},{2,1},{3,2},{4,7},{5,4},{6,5},{7,6},{8,11},{9,8},{10,9... | collective-permute-start | bytes 1179656 | tf_op jit(solution)/shard_map/ppermute | solution.py:418
  81.5 11.9 %collective-permute-start.13 = (f32[3,2,64,256]{3,2,1,0:T(8,128)S(1)}, f32[3,2,64,256]{3,2,1,0:T(8,128)S(1)}, u32[]{:S(2)}, u32[]{:S(2)}) collective-permute-start(f32[3,2,64,256]{3,2,1,0:T(8,128)S(1)} %combine.6), channel_id=1, source_target_pairs={{0,1},{1,2},{2,3},{3,0},{4,5},{5,6},{6,7},{7,4},{8,9},{9,10},{10,1... | collective-permute-start | bytes 1179656 | tf_op jit(solution)/shard_map/ppermute | solution.py:418
  82.3 17.4 %copy-start = (f32[2,256,256]{2,1,0:T(8,128)S(1)}, f32[2,256,256]{2,1,0:T(8,128)}, u32[]{:S(2)}) copy-start(f32[2,256,256]{2,1,0:T(8,128)} %solution.1) | copy-start | bytes 1572868
  82.3 17.4 %collective-permute-start.14 = (f32[3,2,64,256]{3,2,1,0:T(8,128)S(1)}, f32[3,2,64,256]{3,2,1,0:T(8,128)S(1)}, u32[]{:S(2)}, u32[]{:S(2)}) collective-permute-start(f32[3,2,64,256]{3,2,1,0:T(8,128)S(1)} %get-tuple-element.106), channel_id=1, source_target_pairs={{0,2},{1,3},{2,0},{3,1},{4,6},{5,7},{6,4},{7,5},{8,10},{9,11},{10,... | collective-permute-start | bytes 1179656 | tf_op jit(solution)/shard_map/ppermute | solution.py:418
